TPU v7x, 256 devices: a whole 4x4x8 slice. The times are simulated.
256 devices in a mesh: dp: 128 (over y, z, x), head: 2 (over core).
Axes of the slice: x: 4, y: 4, z: 8, core: 2. Of those that a mesh axis runs over, the one named last changes fastest.
Arguments:
- teacher_hidden: bfloat16 [327680, 1024], P('dp', 'head'), may hold values from -6 to 6
- student_hidden: bfloat16 [327680, 312], P('dp'), may hold values from -6 to 6
- projector: bfloat16 [312, 1024], P(None, 'head'), may hold values from -0.3125 to 0.3125
- teacher_queries: bfloat16 [327680, 1024], P('dp', 'head'), may hold values from -6 to 6
- teacher_keys: bfloat16 [327680, 1024], P('dp', 'head'), may hold values from -6 to 6
- student_queries: bfloat16 [327680, 312], P('dp', 'head'), may hold values from -6 to 6
- student_keys: bfloat16 [327680, 312], P('dp', 'head'), may hold values from -6 to 6
- lengths: int32 [640], replicated, may hold values from 32 to 512, as said below
- plan: int32 [7, 128], replicated, may hold values from 0 to 4, as said below
Outputs:
- hidden_row: float32 [327680], P(('dp', 'head'))
- row_loss: float32 [128, 2, 5, 256], P('dp', 'head')
- loss: float32 [], replicated
Inputs may be any that keep to these rules, and one draw needn't show every extreme that they name: lengths[k] counts the real tokens of the sequence in rows k * 512 onward, first held in slot k mod 5 of dp index k // 5; the rows after them are padding. Some sequence has exactly 512 tokens. In round r, dp index d gives the sequence in its slot plan[r, d] to dp index d XOR 2^r and receives that device's slot plan[r, d XOR 2^r] into the same slot; the rounds tend to even out the sum of squared lengths of the devices.
All inputs are finite; a program needn't handle non-finite values.
Results may differ from a plain program's by a relative error of at most 0.0003.
Values may be sent and summed in bfloat16 or wider, within the bound.
A program may use at most 128 MiB of HBM per device.

v0:
```python
import functools
import math

import jax
import jax.numpy as jnp
from jax import lax
from jax.sharding import Mesh
from jax.sharding import PartitionSpec as P

HEADS_T = 16
HEAD_T = 64
HEADS_S = 12
HEAD_S = 26
MAXLEN = 512
D_T = 1024
DP = ("dp_0", "dp_1", "dp_2")
DP_HEAD = ("dp_0", "dp_1", "dp_2", "head")


def cut_along(shard, dim, devices):
    before, after = (shard.shape[:dim], shard.shape[dim + 1 :])
    return jnp.moveaxis(shard.reshape(*before, devices, -1, *after), dim, 0)


def summed_on_arrival(shard, axis, dim):
    blocks = cut_along(shard, dim, lax.axis_size(axis))
    arrived = lax.all_to_all(blocks, axis, split_axis=0, concat_axis=0, tiled=True)
    return arrived.sum(axis=0)


def partner(value, axis, distance):
    mask = 2**distance
    pairs = [(source, source ^ mask) for source in range(lax.axis_size(axis))]
    return lax.ppermute(value, axis, pairs)


def one_axis_at_a_time(shard, axes):
    return functools.reduce(lax.psum, axes, shard)


def select_entry(values, my_index):
    picked = jnp.where(jnp.arange(values.shape[0], dtype=jnp.int32) == my_index, values, 0)
    return jnp.sum(picked)


def select_row(slot_table, my_index):
    picked = jnp.where(
        (jnp.arange(slot_table.shape[0], dtype=jnp.int32) == my_index)[:, None], slot_table, 0
    )
    return jnp.sum(picked, axis=0)


def slot_map(operands, length):
    max_rows = operands[0].shape[0]
    tile_rows = max_rows // 4
    t_scale = 1.0 / (HEADS_T * math.sqrt(HEAD_T))
    s_scale = 1.0 / (HEADS_S * math.sqrt(HEAD_S))

    def make_branch(used_rows):

        def branch(values):
            teach_query, teach_key, pupil_query, pupil_key = values
            teacher_map = jnp.einsum(
                "ic,jc->ij",
                teach_query[:used_rows],
                teach_key[:used_rows],
                preferred_element_type=jnp.float32,
            )
            student_map = jnp.einsum(
                "ic,jc->ij",
                pupil_query[:used_rows],
                pupil_key[:used_rows],
                preferred_element_type=jnp.float32,
            )
            inside = jnp.arange(used_rows, dtype=jnp.int32) < length
            difference = jnp.where(
                inside[:, None] & inside[None, :],
                teacher_map * t_scale - student_map * s_scale,
                0.0,
            )
            return jnp.pad(difference, ((0, max_rows - used_rows), (0, max_rows - used_rows)))

        return branch

    branches = [make_branch((bucket + 1) * tile_rows) for bucket in range(4)]
    bucket_index = (length + tile_rows - 1) // tile_rows - 1
    return lax.switch(bucket_index, branches, operands)


def attention_rows(pieces, slot_lengths):
    slot_count = pieces[0].shape[0]
    full_maps = jnp.stack(
        [
            slot_map(tuple((member[slot_number] for member in pieces)), slot_lengths[slot_number])
            for slot_number in range(slot_count)
        ]
    )
    halves = summed_on_arrival(full_maps, "head", 1)
    squares = halves * halves
    row_losses = jnp.sum(squares, axis=2) / slot_lengths[:, None].astype(jnp.float32)
    return (row_losses, jnp.sum(squares))


def body(
    teacher_hidden,
    student_hidden,
    projector,
    teacher_queries,
    teacher_keys,
    student_queries,
    student_keys,
    lengths,
    plan,
):
    device_count = lax.axis_size(DP)
    my_index = lax.axis_index(DP)
    slot_count = teacher_hidden.shape[0] // MAXLEN
    slot_table = lengths.reshape(device_count, slot_count)
    own_lengths = select_row(slot_table, my_index)
    projected = jnp.dot(student_hidden, projector, preferred_element_type=jnp.float32)
    errors = projected - teacher_hidden.astype(jnp.float32)
    row_part = jnp.sum(errors * errors, axis=1).reshape(slot_count, MAXLEN)
    inside = jnp.arange(MAXLEN, dtype=jnp.int32)[None, :] < own_lengths[:, None]
    row_part = jnp.where(inside, row_part, 0.0).reshape(slot_count * MAXLEN)
    hidden_row = summed_on_arrival(row_part, "head", 0) / D_T
    hidden_local = jnp.sum(hidden_row)
    pieces = (
        teacher_queries.reshape(slot_count, MAXLEN, -1),
        teacher_keys.reshape(slot_count, MAXLEN, -1),
        student_queries.reshape(slot_count, MAXLEN, -1),
        student_keys.reshape(slot_count, MAXLEN, -1),
    )
    row_losses, attention_local = attention_rows(pieces, own_lengths)
    for bit_index in range(plan.shape[0]):
        my_slot = select_entry(plan[bit_index], my_index)
        outgoing = lax.dynamic_index_in_dim(row_losses, my_slot, 0, keepdims=False)
        arrived = partner(outgoing, DP, bit_index)
        row_losses = lax.dynamic_update_index_in_dim(row_losses, arrived, my_slot, 0)
    hidden_total, attention_total = (
        one_axis_at_a_time(hidden_local, DP_HEAD),
        one_axis_at_a_time(attention_local, DP_HEAD),
    )
    lengths_float = lengths.astype(jnp.float32)
    loss = hidden_total / jnp.sum(lengths_float) + attention_total / jnp.sum(
        lengths_float * lengths_float
    )
    return (hidden_row, row_losses.reshape(1, 1, slot_count, row_losses.shape[1]), loss)


def solution(mesh):
    torus = Mesh(
        mesh.devices.reshape(4, 8, 4, mesh.shape["head"]), ("dp_0", "dp_1", "dp_2", "head")
    )
    placed = (
        P(DP, "head"),
        P(DP, None),
        P(None, "head"),
        P(DP, "head"),
        P(DP, "head"),
        P(DP, "head"),
        P(DP, "head"),
        P(),
        P(),
    )
    return jax.shard_map(
        body,
        mesh=torus,
        in_specs=placed,
        out_specs=(P(DP_HEAD), P(DP, "head", None, None), P()),
        check_vma=False,
    )
```

profile of v0, /device:TPU:1, one launch (start us, length us, event | category | flops | bytes accessed | tf_op | source)
XLA Modules:
  0.0 163.0 jit_solution(506503207838221416)
XLA Ops:
  0.7 1.0 reshape.297
  1.8 0.6 fusion.128
  5.5 8.1 %conditional.5 = (f32[1,2,256,512]{3,2,1,0:T(8,128)}) conditional(s32[]{:T(128)} %clamp.15, (s32[]{:T(128)}, bf16[2560,512]{1,0:T(8,128)(2,1)}, bf16[2560,512]{1,0:T(8,128)(2,1)}, bf16[2560,156]{0,1:T(8,128)(2,1)}, bf16[2560,156]{0,1:T(8,128)(2,1)}) %tuple.88, (s32[]{:T(128)}, bf16[2560,512]{1,0:T(8,128)(2,1)}, ...), branch_computations={%region_3.4_spmd, %region_4.5_spmd, %region_5.6_spmd, %region_6.7_... | conditional | flops 351535616 | bytes 11109928 | solution.py:87
  5.5 2.4 %copy.191 = bf16[2560,156]{1,0:T(8,128)(2,1)} copy(bf16[2560,156]{0,1:T(8,128)(2,1)} %get-tuple-element.821) | data formatting | bytes 1597440 | tf_op jit(solution)/shard_map
  8.0 1.4 copy.192
  9.4 1.3 convolution_multiply_fusion.3
  10.7 0.6 iota_compare_fusion.1
  11.3 1.2 fusion.7
  12.5 1.1 pad.34
  13.6 2.4 %bitcast_dynamic-update-slice_fusion.4 = f32[5,2,256,512]{3,2,0,1:T(8,128)} fusion(f32[1,2,256,512]{3,2,1,0:T(8,128)} %get-tuple-element.942), kind=kLoop, calls=%fused_computation.187 | loop fusion | bytes 2097152
  16.0 7.0 %conditional.6 = (f32[1,2,256,512]{3,2,1,0:T(8,128)}) conditional(s32[]{:T(128)} %clamp.16, (s32[]{:T(128)}, bf16[2560,512]{1,0:T(8,128)(2,1)}, bf16[2560,512]{1,0:T(8,128)(2,1)}, bf16[2560,156]{0,1:T(8,128)(2,1)S(1)}, bf16[2560,156]{0,1:T(8,128)(2,1)S(1)}) %tuple.244, (s32[]{:T(128)}, bf16[2560,512]{1,0:T(8,128)(2,1)}, ...), branch_computations={%region_7.8_spmd, %region_8.9_spmd, %region_9.10_spmd, %region_10.... | conditional | flops 351535616 | bytes 7915020 | solution.py:87
  16.0 1.4 copy.199
  17.4 1.4 copy.200
  18.8 1.3 convolution_multiply_fusion.11
  20.1 0.6 iota_compare_fusion.5
  20.7 1.2 fusion.31
  21.9 1.1 pad.37
  23.0 2.3 %bitcast_dynamic-update-slice_fusion.3 = f32[5,2,256,512]{3,2,0,1:T(8,128)} fusion(f32[5,2,256,512]{3,2,0,1:T(8,128)} %bitcast_dynamic-update-slice_fusion.4, f32[1,2,256,512]{3,2,1,0:T(8,128)} %get-tuple-element.943), kind=kLoop, calls=%fused_computation.186 | loop fusion | bytes 2097152
  25.3 6.8 %conditional.7 = (f32[1,2,256,512]{3,2,1,0:T(8,128)}) conditional(s32[]{:T(128)} %clamp.17, (s32[]{:T(128)}, bf16[2560,512]{1,0:T(8,128)(2,1)}, bf16[2560,512]{1,0:T(8,128)(2,1)}, bf16[2560,156]{0,1:T(8,128)(2,1)S(1)}, bf16[2560,156]{0,1:T(8,128)(2,1)S(1)}) %tuple.248, (s32[]{:T(128)}, bf16[2560,512]{1,0:T(8,128)(2,1)}, ...), branch_computations={%region_11.12_spmd, %region_12.13_spmd, %region_13.14_spmd, %regio... | conditional | flops 351535616 | bytes 7915020 | solution.py:87
  25.3 1.4 copy.205
  26.7 1.4 copy.206
  28.1 1.2 convolution_multiply_fusion.17
  29.3 0.7 iota_compare_fusion.8
  29.9 1.0 fusion.49
  31.0 1.1 pad.39
  32.1 2.3 %bitcast_dynamic-update-slice_fusion.2 = f32[5,2,256,512]{3,2,0,1:T(8,128)} fusion(f32[5,2,256,512]{3,2,0,1:T(8,128)} %bitcast_dynamic-update-slice_fusion.3, f32[1,2,256,512]{3,2,1,0:T(8,128)} %get-tuple-element.944), kind=kLoop, calls=%fused_computation.185 | loop fusion | bytes 2097152
  34.4 7.1 %conditional.8 = (f32[1,2,256,512]{3,2,1,0:T(8,128)}) conditional(s32[]{:T(128)} %clamp.18, (s32[]{:T(128)}, bf16[2560,512]{1,0:T(8,128)(2,1)}, bf16[2560,512]{1,0:T(8,128)(2,1)}, bf16[2560,156]{0,1:T(8,128)(2,1)S(1)}, bf16[2560,156]{0,1:T(8,128)(2,1)S(1)}) %tuple.252, (s32[]{:T(128)}, bf16[2560,512]{1,0:T(8,128)(2,1)}, ...), branch_computations={%region_15.16_spmd, %region_16.17_spmd, %region_17.18_spmd, %regio... | conditional | flops 351535616 | bytes 7915020 | solution.py:87
  34.4 1.4 copy.215
  35.8 1.4 copy.216
  37.2 1.3 convolution_multiply_fusion.27
  38.5 0.7 iota_compare_fusion.13
  39.2 1.2 fusion.79
  40.4 1.1 pad.43
  41.5 2.3 %bitcast_dynamic-update-slice_fusion.1 = f32[5,2,256,512]{3,2,0,1:T(8,128)} fusion(f32[5,2,256,512]{3,2,0,1:T(8,128)} %bitcast_dynamic-update-slice_fusion.2, f32[1,2,256,512]{3,2,1,0:T(8,128)} %get-tuple-element.945), kind=kLoop, calls=%fused_computation.184 | loop fusion | bytes 2097152
  43.8 5.8 %conditional.9 = (f32[1,2,256,512]{3,2,1,0:T(8,128)S(1)}) conditional(s32[]{:T(128)} %clamp.19, (s32[]{:T(128)}, bf16[2560,512]{1,0:T(8,128)(2,1)}, bf16[2560,512]{1,0:T(8,128)(2,1)}, bf16[2560,156]{0,1:T(8,128)(2,1)S(1)}, bf16[2560,156]{0,1:T(8,128)(2,1)S(1)}) %tuple.256, (s32[]{:T(128)}, ...), branch_computations={%region_19.20_spmd, %region_20.21_spmd, %region_21.22_spmd, %regio... | conditional | flops 351535616 | bytes 7915020 | solution.py:87
  43.8 1.4 copy.221
  45.2 1.4 copy.222
  46.6 1.2 convolution_multiply_fusion.33
  47.8 0.7 iota_compare_fusion.16
  48.5 1.0 fusion.97
  49.7 1.1 bitcast_dynamic-update-slice_fusion
  50.7 9.1 %all-to-all-start.1 = ((f32[2,5,256,512]{3,2,1,0:T(8,128)}), f32[2,5,256,512]{3,2,1,0:T(8,128)}, u32[]{:S(2)}, u32[]{:S(2)}) async-start(f32[2,5,256,512]{3,2,1,0:T(8,128)} %bitcast.81), calls=%async_computation.1 | async-start | bytes 10485760 | tf_op jit(solution)/shard_map/all_to_all | solution.py:27
  59.9 4.9 %all-to-all-done.1 = f32[2,5,256,512]{3,2,1,0:T(8,128)} async-done(((f32[2,5,256,512]{3,2,1,0:T(8,128)}), f32[2,5,256,512]{3,2,1,0:T(8,128)}, u32[]{:S(2)}, u32[]{:S(2)}) %all-to-all-start.1) | async-done | bytes 5242912 | tf_op jit(solution)/shard_map/all_to_all | solution.py:27
  64.8 4.9 %reduce_sum.147 = f32[5,256,512]{2,1,0:T(8,128)} reduce(f32[2,5,256,512]{3,2,1,0:T(8,128)} %all-to-all-done.1, f32[]{:T(128)} %constant.267.clone.1), dimensions={0}, to_apply=%region_23.24 | reduce | flops 655360 | bytes 7864324 | tf_op jit(solution)/shard_map/reduce_sum | solution.py:28
  69.6 3.1 %multiply_reduce_fusion.1 = (f32[]{:T(128)}, f32[5,256]{1,0:T(8,128)S(1)}) fusion(f32[5,256,512]{2,1,0:T(8,128)} %reduce_sum.147), kind=kLoop, calls=%fused_computation.181 | loop fusion | flops 1964799 | bytes 2626564 | tf_op jit(solution)/shard_map/reduce_sum | solution.py:101
  72.7 0.8 fusion.120
  75.3 0.5 collective-permute-start
  78.0 3.0 %collective-permute-start.1 = (f32[256]{0:T(256)S(1)}, f32[256]{0:T(256)S(1)}, u32[]{:S(2)}, u32[]{:S(2)}) collective-permute-start(f32[256]{0:T(256)S(1)} %bitcast.110), channel_id=1, source_target_pairs={{0,4},{2,6},{4,0},{6,2},{8,12},{10,14},{12,8},{14,10},{16,20},{18,... | collective-permute-start | bytes 3080 | tf_op jit(solution)/shard_map/ppermute | solution.py:34
  82.1 4.4 %copy.187 = bf16[2560,512]{0,1:T(8,128)(2,1)} copy(bf16[2560,512]{1,0:T(8,128)(2,1)} %param.29) | data formatting | bytes 5242880 | tf_op args[0]
  87.2 1.6 %collective-permute-start.2 = (f32[256]{0:T(256)S(1)}, f32[256]{0:T(256)S(1)}, u32[]{:S(2)}, u32[]{:S(2)}) collective-permute-start(f32[256]{0:T(256)S(1)} %bitcast.109), channel_id=1, source_target_pairs={{0,8},{2,10},{4,12},{6,14},{8,0},{10,2},{12,4},{14,6},{16,24},{18,... | collective-permute-start | bytes 3080 | tf_op jit(solution)/shard_map/ppermute | solution.py:34
  88.8 3.5 %multiply_reduce_fusion = f32[2560]{0:T(1024)S(1)} fusion(bf16[2560,512]{0,1:T(8,128)(2,1)} %copy.187, bf16[2560,312]{0,1:T(8,128)(2,1)S(1)} %copy-done, bf16[312,512]{1,0:T(8,128)(2,1)S(1)} %copy-done.9), kind=kOutput, calls=%fused_computation.180 | convolution fusion | flops 823129600 | bytes 4548608 | tf_op jit(solution)/shard_map/dot_general | solution.py:120
  94.3 4.0 %collective-permute-start.3 = (f32[256]{0:T(256)S(1)}, f32[256]{0:T(256)S(1)}, u32[]{:S(2)}, u32[]{:S(2)}) collective-permute-start(f32[256]{0:T(256)S(1)} %bitcast.107), channel_id=1, source_target_pairs={{0,16},{2,18},{4,20},{6,22},{8,24},{10,26},{12,28},{14,30},{16,0},... | collective-permute-start | bytes 3080 | tf_op jit(solution)/shard_map/ppermute | solution.py:34
  100.4 4.7 %collective-permute-start.4 = (f32[256]{0:T(256)S(1)}, f32[256]{0:T(256)S(1)}, u32[]{:S(2)}, u32[]{:S(2)}) collective-permute-start(f32[256]{0:T(256)S(1)} %bitcast.106), channel_id=1, source_target_pairs={{0,32},{2,34},{4,36},{6,38},{8,40},{10,42},{12,44},{14,46},{16,48}... | collective-permute-start | bytes 3080 | tf_op jit(solution)/shard_map/ppermute | solution.py:34
  105.2 0.6 copy.188
  105.8 5.0 %all-to-all-start = ((f32[2,1,1280]{2,1,0:T(1,128)}), f32[2,1,1280]{2,1,0:T(1,128)S(1)}, u32[]{:S(2)}, u32[]{:S(2)}) async-start(f32[2,1,1280]{2,1,0:T(1,128)} %copy.188), calls=%async_computation | async-start | bytes 20480 | tf_op jit(solution)/shard_map/all_to_all | solution.py:27
  112.8 1.8 %collective-permute-start.5 = (f32[256]{0:T(256)S(1)}, f32[256]{0:T(256)S(1)}, u32[]{:S(2)}, u32[]{:S(2)}) collective-permute-start(f32[256]{0:T(256)S(1)} %bitcast.108), channel_id=1, source_target_pairs={{0,64},{2,66},{4,68},{6,70},{8,72},{10,74},{12,76},{14,78},{16,80}... | collective-permute-start | bytes 3080 | tf_op jit(solution)/shard_map/ppermute | solution.py:34
  114.6 1.2 fusion.127
  117.7 3.1 %collective-permute-start.6 = (f32[256]{0:T(256)S(1)}, f32[256]{0:T(256)S(1)}, u32[]{:S(2)}, u32[]{:S(2)}) collective-permute-start(f32[256]{0:T(256)S(1)} %bitcast.105), channel_id=1, source_target_pairs={{0,128},{2,130},{4,132},{6,134},{8,136},{10,138},{12,140},{14,142}... | collective-permute-start | bytes 3080 | tf_op jit(solution)/shard_map/ppermute | solution.py:34
  120.9 0.7 multiply_reduce_fusion.3
  121.6 6.9 %all-reduce.17 = (f32[]{:T(128)}, f32[]{:T(128)}) all-reduce(f32[]{:T(128)} %get-tuple-element.935, f32[]{:T(128)} %get-tuple-element.916), channel_id=1, replica_groups=mesh['dp_0'=4,'dp_1'=8,'dp_2'=4,'head'=2] {'dp_0'}, use_global_device_ids=true, to_apply=%region_33.34 | all-reduce | flops 2 | bytes 16 | tf_op jit(solution)/shard_map/psum | solution.py:38
  128.5 11.6 %all-reduce.15 = (f32[]{:T(128)}, f32[]{:T(128)}) all-reduce(f32[]{:T(128)} %get-tuple-element.931, f32[]{:T(128)} %get-tuple-element.932), channel_id=1, replica_groups=mesh['dp_0'=4,'dp_1'=8,'dp_2'=4,'head'=2] {'dp_1'}, use_global_device_ids=true, to_apply=%region_34.35 | all-reduce | flops 2 | bytes 16 | tf_op jit(solution)/shard_map/psum | solution.py:38
  140.1 7.7 %all-reduce.16 = (f32[]{:T(128)}, f32[]{:T(128)}) all-reduce(f32[]{:T(128)} %get-tuple-element.927, f32[]{:T(128)} %get-tuple-element.928), channel_id=1, replica_groups=mesh['dp_0'=4,'dp_1'=8,'dp_2'=4,'head'=2] {'dp_2'}, use_global_device_ids=true, to_apply=%region_35.36 | all-reduce | flops 2 | bytes 16 | tf_op jit(solution)/shard_map/psum | solution.py:38
  147.8 10.8 %all-reduce.18 = (f32[]{:T(128)}, f32[]{:T(128)}) all-reduce(f32[]{:T(128)} %get-tuple-element.929, f32[]{:T(128)} %get-tuple-element.930), channel_id=1, replica_groups=mesh['dp_0'=4,'dp_1'=8,'dp_2'=4,'head'=2] {'head'}, use_global_device_ids=true, to_apply=%region_36.37 | all-reduce | flops 2 | bytes 16 | tf_op jit(solution)/shard_map/psum | solution.py:38
  161.3 0.6 copy.234
  (46 shorter events, 0.9 us)
Async XLA Ops:
  0.6 88.2 %copy-start = (bf16[2560,312]{0,1:T(8,128)(2,1)S(1)}, bf16[2560,312]{0,1:T(8,128)(2,1)}, u32[]{:S(2)}) copy-start(bf16[2560,312]{0,1:T(8,128)(2,1)} %param.30) | copy-start | bytes 4792324
  5.5 2.4 %copy-start.4 = (bf16[2560,156]{0,1:T(8,128)(2,1)S(1)}, bf16[2560,156]{0,1:T(8,128)(2,1)}, u32[]{:S(2)}) copy-start(bf16[2560,156]{0,1:T(8,128)(2,1)} %get-tuple-element.822) | copy-start | bytes 2396164 | tf_op jit(solution)/shard_map/cond
  13.6 2.4 %copy-start.1 = (bf16[2560,156]{0,1:T(8,128)(2,1)S(1)}, bf16[2560,156]{0,1:T(8,128)(2,1)}, u32[]{:S(2)}) copy-start(bf16[2560,156]{0,1:T(8,128)(2,1)} %param.34) | copy-start | bytes 2396164
  13.6 2.4 %copy-start.2 = (bf16[2560,156]{0,1:T(8,128)(2,1)S(1)}, bf16[2560,156]{0,1:T(8,128)(2,1)}, u32[]{:S(2)}) copy-start(bf16[2560,156]{0,1:T(8,128)(2,1)} %param.35) | copy-start | bytes 2396164
  50.7 14.0 %all-to-all-start.1 = ((f32[2,5,256,512]{3,2,1,0:T(8,128)}), f32[2,5,256,512]{3,2,1,0:T(8,128)}, u32[]{:S(2)}, u32[]{:S(2)}) async-start(f32[2,5,256,512]{3,2,1,0:T(8,128)} %bitcast.81), calls=%async_computation.1 | async-start | bytes 10485760 | tf_op jit(solution)/shard_map/all_to_all | solution.py:27
  69.6 3.1 %copy-start.8 = (s32[7,128]{1,0:T(8,128)S(1)}, s32[7,128]{1,0:T(8,128)}, u32[]{:S(2)}) copy-start(s32[7,128]{1,0:T(8,128)} %param.37) | copy-start | bytes 10756
  75.3 2.6 %collective-permute-start = (f32[256]{0:T(256)S(1)}, f32[256]{0:T(256)S(1)}, u32[]{:S(2)}, u32[]{:S(2)}) collective-permute-start(f32[256]{0:T(256)S(1)} %bitcast.111), channel_id=1, source_target_pairs={{0,2},{2,0},{4,6},{6,4},{8,10},{10,8},{12,14},{14,12},{16,18},{18,... | collective-permute-start | bytes 3080 | tf_op jit(solution)/shard_map/ppermute | solution.py:34
  78.0 9.1 %collective-permute-start.1 = (f32[256]{0:T(256)S(1)}, f32[256]{0:T(256)S(1)}, u32[]{:S(2)}, u32[]{:S(2)}) collective-permute-start(f32[256]{0:T(256)S(1)} %bitcast.110), channel_id=1, source_target_pairs={{0,4},{2,6},{4,0},{6,2},{8,12},{10,14},{12,8},{14,10},{16,20},{18,... | collective-permute-start | bytes 3080 | tf_op jit(solution)/shard_map/ppermute | solution.py:34
  82.1 6.7 %copy-start.9 = (bf16[312,512]{1,0:T(8,128)(2,1)S(1)}, bf16[312,512]{1,0:T(8,128)(2,1)}, u32[]{:S(2)}) copy-start(bf16[312,512]{1,0:T(8,128)(2,1)} %param.31) | copy-start | bytes 958468
  87.2 33.7 %copy-start.7 = (s32[640]{0:T(1024)S(1)}, s32[640]{0:T(1024)}, u32[]{:S(2)}) copy-start(s32[640]{0:T(1024)} %param.36) | copy-start | bytes 7684
  87.2 7.1 %collective-permute-start.2 = (f32[256]{0:T(256)S(1)}, f32[256]{0:T(256)S(1)}, u32[]{:S(2)}, u32[]{:S(2)}) collective-permute-start(f32[256]{0:T(256)S(1)} %bitcast.109), channel_id=1, source_target_pairs={{0,8},{2,10},{4,12},{6,14},{8,0},{10,2},{12,4},{14,6},{16,24},{18,... | collective-permute-start | bytes 3080 | tf_op jit(solution)/shard_map/ppermute | solution.py:34
  94.3 6.0 %collective-permute-start.3 = (f32[256]{0:T(256)S(1)}, f32[256]{0:T(256)S(1)}, u32[]{:S(2)}, u32[]{:S(2)}) collective-permute-start(f32[256]{0:T(256)S(1)} %bitcast.107), channel_id=1, source_target_pairs={{0,16},{2,18},{4,20},{6,22},{8,24},{10,26},{12,28},{14,30},{16,0},... | collective-permute-start | bytes 3080 | tf_op jit(solution)/shard_map/ppermute | solution.py:34
  100.4 12.3 %collective-permute-start.4 = (f32[256]{0:T(256)S(1)}, f32[256]{0:T(256)S(1)}, u32[]{:S(2)}, u32[]{:S(2)}) collective-permute-start(f32[256]{0:T(256)S(1)} %bitcast.106), channel_id=1, source_target_pairs={{0,32},{2,34},{4,36},{6,38},{8,40},{10,42},{12,44},{14,46},{16,48}... | collective-permute-start | bytes 3080 | tf_op jit(solution)/shard_map/ppermute | solution.py:34
  105.8 6.9 %all-to-all-start = ((f32[2,1,1280]{2,1,0:T(1,128)}), f32[2,1,1280]{2,1,0:T(1,128)S(1)}, u32[]{:S(2)}, u32[]{:S(2)}) async-start(f32[2,1,1280]{2,1,0:T(1,128)} %copy.188), calls=%async_computation | async-start | bytes 20480 | tf_op jit(solution)/shard_map/all_to_all | solution.py:27
  112.8 4.8 %collective-permute-start.5 = (f32[256]{0:T(256)S(1)}, f32[256]{0:T(256)S(1)}, u32[]{:S(2)}, u32[]{:S(2)}) collective-permute-start(f32[256]{0:T(256)S(1)} %bitcast.108), channel_id=1, source_target_pairs={{0,64},{2,66},{4,68},{6,70},{8,72},{10,74},{12,76},{14,78},{16,80}... | collective-permute-start | bytes 3080 | tf_op jit(solution)/shard_map/ppermute | solution.py:34
  117.7 43.5 %collective-permute-start.6 = (f32[256]{0:T(256)S(1)}, f32[256]{0:T(256)S(1)}, u32[]{:S(2)}, u32[]{:S(2)}) collective-permute-start(f32[256]{0:T(256)S(1)} %bitcast.105), channel_id=1, source_target_pairs={{0,128},{2,130},{4,132},{6,134},{8,136},{10,138},{12,140},{14,142}... | collective-permute-start | bytes 3080 | tf_op jit(solution)/shard_map/ppermute | solution.py:34
where the time goes:
time: 164 us; the launch traced here: 163 us
  local copies, waits for them, and re-layouts  37.8 us (23%)
  blocking collectives  37.1 us (23%)
  starting transfers between devices  32.9 us (20%)
  between operations  20.9 us (13%)
  matrix products  15.3 us (9%)
  other arithmetic  14 us (9%)
  waiting for transfers between devices  4.9 us (3%)
    psum x4, blocking collectives, one_axis_at_a_time(): return functools.reduce(lax.psum, axes, shard)  37.1 us
    ppermute x7, starting transfers between devices, partner(): return lax.ppermute(value, axis, pairs)  18.8 us
    another operation x10, local copies, waits for them, and re-layouts  15.1 us
    unnamed x18, local copies, waits for them, and re-layouts  14.3 us
    all_to_all x2, starting transfers between devices, summed_on_arrival(): lax.all_to_all(blocks, axis, split_axis=0, concat_axis=0, tiled=True)  14.1 us
    dot_general x5, matrix products, branch(): jnp.einsum('ic,jc->ij', teach_query[:used_rows], teach_key[:used_rows], p...  6.17 us
    dot_general x5, matrix products, branch(): jnp.einsum('ic,jc->ij', pupil_query[:used_rows], pupil_key[:used_rows], p...  5.69 us
    reduce_sum x2, other arithmetic, summed_on_arrival(): return arrived.sum(axis=0)  4.88 us
  transfers between devices with their start and end apart: 9, of which 1 were waited for; matrix products, arithmetic and copies ran while one was open for 6% of the time, Pallas kernels for 0%

commit v1 on v0

v1 whole, which is shorter than its diff:
```python
import functools
import math

import jax
import jax.numpy as jnp
from jax import lax
from jax.experimental import pallas as pl
from jax.experimental.pallas import tpu as pltpu
from jax.sharding import Mesh
from jax.sharding import PartitionSpec as P

HEADS_T = 16
HEAD_T = 64
HEADS_S = 12
HEAD_S = 26
MAXLEN = 512
HALF = 256
SLOTS = 5
D_T = 1024
DP = ("dp_0", "dp_1", "dp_2")
DP_HEAD = ("dp_0", "dp_1", "dp_2", "head")
MESH = pl.DeviceIdType.MESH

T_SCALE = 1.0 / (HEADS_T * math.sqrt(HEAD_T))
S_SCALE = 1.0 / (HEADS_S * math.sqrt(HEAD_S))
KAPPA = S_SCALE / T_SCALE
OUT_SCALE = T_SCALE * T_SCALE


def flip(device, bit):
    mask = 2**bit
    return device + mask * (1 - 2 * ((device // mask) % 2))


def trace_forward(plan, device, slot, bits):
    for bit in bits:
        other = flip(device, bit)
        moves = plan[bit, device] == slot
        slot = jnp.where(moves, plan[bit, other], slot)
        device = jnp.where(moves, other, device)
    return device, slot


def trace_backward(plan, device, slot, bits):
    return trace_forward(plan, device, slot, tuple(reversed(bits)))


def kernel(
    sizes,
    bits,
    th,
    sht,
    pj,
    tq,
    tk,
    sqt,
    skt,
    lens,
    plan,
    hid_out,
    row_out,
    loss_out,
    tk_v,
    tq_v,
    sk_v,
    sq_v,
    th_v,
    sh_v,
    pj_v,
    len_v,
    len_s,
    plan_s,
    map_send,
    map_own,
    map_recv,
    hid_send,
    hid_recv,
    send_x,
    send_z,
    send_y,
    recv_x,
    recv_z,
    recv_y,
    cross_y,
    rows_x,
    rows_z,
    rows_y,
    load_sem,
    small_sem,
    map_ssem,
    map_rsem,
    hid_sem,
    ssem_x,
    rsem_x,
    ssem_z,
    rsem_z,
    ssem_y,
    rsem_y,
    ssem_c,
    rsem_c,
):
    ny, nz, nx = sizes
    y, z, x = (lax.axis_index(name) for name in DP)
    head = lax.axis_index("head")
    away = 1 - head
    me = (y * nz + z) * nx + x

    small = [
        pltpu.make_async_copy(plan, plan_s, small_sem.at[0]),
        pltpu.make_async_copy(lens, len_s, small_sem.at[1]),
        pltpu.make_async_copy(lens, len_v, small_sem.at[2]),
    ]
    loads = []
    for s in range(SLOTS):
        own = pl.multiple_of(s * MAXLEN + head * HALF, HALF)
        oth = pl.multiple_of(s * MAXLEN + away * HALF, HALF)
        n = 6 * s
        loads.append(
            [
                pltpu.make_async_copy(tk.at[pl.ds(s * MAXLEN, MAXLEN)], tk_v.at[s], load_sem.at[n]),
                pltpu.make_async_copy(tq.at[pl.ds(oth, HALF)], tq_v.at[s, 0], load_sem.at[n + 1]),
                pltpu.make_async_copy(
                    skt.at[:, pl.ds(s * MAXLEN, MAXLEN)], sk_v.at[s], load_sem.at[n + 2]
                ),
                pltpu.make_async_copy(sqt.at[:, pl.ds(oth, HALF)], sq_v.at[s, 0], load_sem.at[n + 3]),
                pltpu.make_async_copy(tq.at[pl.ds(own, HALF)], tq_v.at[s, 1], load_sem.at[n + 4]),
                pltpu.make_async_copy(sqt.at[:, pl.ds(own, HALF)], sq_v.at[s, 1], load_sem.at[n + 5]),
            ]
        )
    base = 6 * SLOTS
    load_pj = pltpu.make_async_copy(pj, pj_v, load_sem.at[base])
    hid_loads = []
    for b in range(2 * SLOTS):
        half = away if b < SLOTS else head
        first = pl.multiple_of((half * SLOTS + b % SLOTS) * HALF, HALF)
        n = base + 1 + 2 * b
        hid_loads.append(
            [
                pltpu.make_async_copy(sht.at[:, pl.ds(first, HALF)], sh_v.at[b], load_sem.at[n]),
                pltpu.make_async_copy(th.at[pl.ds(first, HALF)], th_v.at[b], load_sem.at[n + 1]),
            ]
        )
    for copy in loads[0]:
        copy.start()
    for copy in small:
        copy.start()
    for s in range(1, SLOTS):
        for copy in loads[s]:
            copy.start()
    load_pj.start()
    for pair in hid_loads:
        for copy in pair:
            copy.start()

    peers = [{"head": away}]
    peers += [{"dp_2": (x + k) % nx} for k in range(1, nx)]
    peers += [{"dp_1": (z + k) % nz} for k in range(1, nz)]
    peers += [{"dp_0": (y + k) % ny} for k in range(1, ny)]
    peers += [{"dp_0": (y + k) % ny, "head": away} for k in range(1, ny)]
    barrier = pltpu.get_barrier_semaphore()
    for peer in peers:
        pl.semaphore_signal(barrier, inc=1, device_id=peer, device_id_type=MESH)

    for copy in small:
        copy.wait()

    def length_of(slot):
        index = me * SLOTS + slot
        return len_s[index // 128, index % 128]

    coords = (x, z, y)
    strides = (1, nx, nx * nz)
    counts = (nx, nz, ny)
    gives, takes = [], []
    for coord, stride, count, rounds in zip(coords, strides, counts, bits):
        lands = [trace_forward(plan_s, me, s, rounds)[0] for s in range(SLOTS)]
        give = []
        for k in range(1, count):
            target = me + stride * ((coord + k) % count - coord)
            slot = jnp.int32(0)
            for s in range(SLOTS):
                slot = jnp.where(lands[s] == target, s, slot)
            give.append(slot)
        gives.append(give)
        take = []
        for s in range(SLOTS):
            device, slot = trace_backward(plan_s, me, s, rounds)
            source = (device // stride) % count
            take.append(jnp.where(device == me, 2 * count + slot, 2 * source))
        takes.append(take)

    def partial_map(s, half):
        teacher = lax.dot_general(
            tk_v[s], tq_v[s, half], (((1,), (1,)), ((), ())), preferred_element_type=jnp.float32
        )
        student = lax.dot_general(
            sk_v[s], sq_v[s, half], (((0,), (0,)), ((), ())), preferred_element_type=jnp.float32
        )
        return teacher - KAPPA * student

    map_copies = []
    for s in range(SLOTS):
        for copy in loads[s]:
            copy.wait()
        map_send[s] = partial_map(s, 0)
        if s == 0:
            pl.semaphore_wait(barrier, len(peers))
        copy = pltpu.make_async_remote_copy(
            src_ref=map_send.at[s],
            dst_ref=map_recv.at[s],
            send_sem=map_ssem.at[s],
            recv_sem=map_rsem.at[s],
            device_id={"head": away},
            device_id_type=MESH,
        )
        copy.start()
        map_copies.append(copy)
        map_own[s] = partial_map(s, 1)

    load_pj.wait()
    lane = lax.broadcasted_iota(jnp.int32, (1, HALF), 1)

    def hidden_block(b):
        for copy in hid_loads[b]:
            copy.wait()
        projected = lax.dot_general(
            sh_v[b], pj_v[...], (((0,), (0,)), ((), ())), preferred_element_type=jnp.float32
        )
        errors = projected - th_v[b].astype(jnp.float32)
        squares = errors * errors
        folded = squares[:, :128]
        for c in range(128, squares.shape[1], 128):
            folded = folded + squares[:, c : c + 128]
        sums = jnp.sum(folded.T, axis=0, keepdims=True)
        half = away if b < SLOTS else head
        block = half * SLOTS + b % SLOTS
        inside = lane + (block % 2) * HALF < length_of(block // 2)
        return jnp.where(inside, sums, 0.0)

    for b in range(SLOTS):
        hid_send[b] = hidden_block(b)
    hid_copy = pltpu.make_async_remote_copy(
        src_ref=hid_send,
        dst_ref=hid_recv,
        send_sem=hid_sem.at[0],
        recv_sem=hid_sem.at[1],
        device_id={"head": away},
        device_id_type=MESH,
    )
    hid_copy.start()
    own_hidden = [hidden_block(SLOTS + b) for b in range(SLOTS)]

    row_iota = lax.broadcasted_iota(jnp.int32, (8, HALF), 0)
    attention = jnp.zeros((1, HALF), jnp.float32)
    for s in range(SLOTS):
        map_copies[s].wait_recv()
        length = length_of(s)
        acc = jnp.zeros((8, HALF), jnp.float32)

        def chunk(c, acc, s=s, length=length):
            first = pl.multiple_of(c * 64, 64)
            whole = map_own[s, pl.ds(first, 64), :] + map_recv[s, pl.ds(first, 64), :]
            for r in range(8):
                part = whole[8 * r : 8 * r + 8, :]
                part = jnp.where(row_iota + (first + 8 * r) < length, part, 0.0)
                acc = acc + part * part
            return acc

        acc = lax.fori_loop(0, MAXLEN // 64, chunk, acc)
        sums = jnp.sum(acc, axis=0, keepdims=True) * OUT_SCALE
        sums = jnp.where(lane + head * HALF < length, sums, 0.0)
        attention = attention + sums
        rows_x[s] = sums / length.astype(jnp.float32)

    hid_copy.wait_recv()
    hidden = jnp.zeros((1, HALF), jnp.float32)
    for b in range(SLOTS):
        total = (own_hidden[b] + hid_recv[b]) * (1.0 / D_T)
        hid_out[2 * b : 2 * b + 1, :] = total[:, :128]
        hid_out[2 * b + 1 : 2 * b + 2, :] = total[:, 128:]
        hidden = hidden + total

    totals = jnp.concatenate(
        [hidden[:, :128] + hidden[:, 128:], attention[:, :128] + attention[:, 128:]], axis=1
    )

    def exchange(axis, coord, count, totals, rows, buffer, send, ssem, rsem, give):
        copies = []
        for k in range(1, count):
            send[2 * (k - 1)] = rows[give[k - 1]]
            send[2 * (k - 1) + 1] = totals
            copies.append(
                pltpu.make_async_remote_copy(
                    src_ref=send.at[pl.ds(2 * (k - 1), 2)],
                    dst_ref=buffer.at[pl.ds(2 * coord, 2)],
                    send_sem=ssem.at[k - 1],
                    recv_sem=rsem.at[k - 1],
                    device_id={axis: (coord + k) % count},
                    device_id_type=MESH,
                )
            )
            copies[-1].start()
        buffer[2 * coord + 1] = totals
        for s in range(SLOTS):
            buffer[2 * count + s] = rows[s]
        return copies

    def summed(rows):
        return functools.reduce(lambda a, b: a + b, rows)

    x_copies = exchange("dp_2", x, nx, totals, rows_x, recv_x, send_x, ssem_x, rsem_x, gives[0])
    for copy in x_copies:
        copy.wait_recv()
    for s in range(SLOTS):
        rows_z[s] = recv_x[takes[0][s]]
    totals = summed([recv_x[2 * i + 1] for i in range(nx)])

    z_copies = exchange("dp_1", z, nz, totals, rows_z, recv_z, send_z, ssem_z, rsem_z, gives[1])
    for copy in z_copies:
        copy.wait_recv()
    for s in range(SLOTS):
        rows_y[s] = recv_z[takes[1][s]]
    totals = summed([recv_z[2 * i + 1] for i in range(nz)])

    y_copies = exchange("dp_0", y, ny, totals, rows_y, recv_y, send_y, ssem_y, rsem_y, gives[2])
    crosses = []
    for k in range(ny):
        copy = pltpu.make_async_remote_copy(
            src_ref=send_y.at[pl.ds(1, 1)],
            dst_ref=cross_y.at[pl.ds(y, 1)],
            send_sem=ssem_c.at[k],
            recv_sem=rsem_c.at[k],
            device_id={"dp_0": (y + k) % ny, "head": away},
            device_id_type=MESH,
        )
        copy.start()
        crosses.append(copy)
    counted = len_v[...].astype(jnp.float32)
    tokens = jnp.sum(jnp.sum(counted, axis=0, keepdims=True), axis=1, keepdims=True)
    pairs = jnp.sum(jnp.sum(counted * counted, axis=0, keepdims=True), axis=1, keepdims=True)
    for copy in y_copies:
        copy.wait_recv()
    for s in range(SLOTS):
        row = recv_y[takes[2][s]]
        row_out[2 * s : 2 * s + 1, :] = row[:, :128]
        row_out[2 * s + 1 : 2 * s + 2, :] = row[:, 128:]
    for copy in crosses:
        copy.wait_recv()
    same = summed([recv_y[2 * i + 1] for i in range(ny)])
    cross = summed([cross_y[i] for i in range(ny)])
    totals = same + cross
    hidden_total = jnp.sum(totals[:, :128], axis=1, keepdims=True)
    attention_total = jnp.sum(totals[:, 128:], axis=1, keepdims=True)
    loss = hidden_total / tokens + attention_total / pairs
    loss_out[...] = jnp.broadcast_to(loss, loss_out.shape)

    for copy in map_copies + [hid_copy] + x_copies + z_copies + y_copies + crosses:
        copy.wait_send()


def body(sizes, bits, th, sh, pj, tq, tk, sq, sk, lengths, plan):
    ny, nz, nx = sizes
    rows = th.shape[0]
    d_s = sh.shape[1]
    half_t, half_s = tq.shape[1], sq.shape[1]
    bf16, f32 = jnp.bfloat16, jnp.float32
    table = lengths.reshape(-1, 128)
    any_spec = pl.BlockSpec(memory_space=pl.ANY)
    vmem_spec = pl.BlockSpec(memory_space=pltpu.VMEM)
    dma = pltpu.SemaphoreType.DMA
    scratch = [
        pltpu.VMEM((SLOTS, MAXLEN, half_t), bf16),
        pltpu.VMEM((SLOTS, 2, HALF, half_t), bf16),
        pltpu.VMEM((SLOTS, half_s, MAXLEN), bf16),
        pltpu.VMEM((SLOTS, 2, half_s, HALF), bf16),
        pltpu.VMEM((2 * SLOTS, HALF, half_t), bf16),
        pltpu.VMEM((2 * SLOTS, d_s, HALF), bf16),
        pltpu.VMEM((d_s, half_t), bf16),
        pltpu.VMEM(table.shape, jnp.int32),
        pltpu.SMEM(table.shape, jnp.int32),
        pltpu.SMEM(plan.shape, jnp.int32),
        pltpu.VMEM((SLOTS, MAXLEN, HALF), f32),
        pltpu.VMEM((SLOTS, MAXLEN, HALF), f32),
        pltpu.VMEM((SLOTS, MAXLEN, HALF), f32),
        pltpu.VMEM((SLOTS, 1, HALF), f32),
        pltpu.VMEM((SLOTS, 1, HALF), f32),
        pltpu.VMEM((2 * (nx - 1), 1, HALF), f32),
        pltpu.VMEM((2 * (nz - 1), 1, HALF), f32),
        pltpu.VMEM((2 * (ny - 1), 1, HALF), f32),
        pltpu.VMEM((2 * nx + SLOTS, 1, HALF), f32),
        pltpu.VMEM((2 * nz + SLOTS, 1, HALF), f32),
        pltpu.VMEM((2 * ny + SLOTS, 1, HALF), f32),
        pltpu.VMEM((ny, 1, HALF), f32),
        pltpu.VMEM((SLOTS, 1, HALF), f32),
        pltpu.VMEM((SLOTS, 1, HALF), f32),
        pltpu.VMEM((SLOTS, 1, HALF), f32),
        dma((6 * SLOTS + 1 + 4 * SLOTS,)),
        dma((3,)),
        dma((SLOTS,)),
        dma((SLOTS,)),
        dma((2,)),
        dma((nx - 1,)),
        dma((nx - 1,)),
        dma((nz - 1,)),
        dma((nz - 1,)),
        dma((ny - 1,)),
        dma((ny - 1,)),
        dma((ny,)),
        dma((ny,)),
    ]
    hid, row, loss = pl.pallas_call(
        functools.partial(kernel, sizes, bits),
        name="distill",
        out_shape=(
            jax.ShapeDtypeStruct((2 * SLOTS, 128), f32),
            jax.ShapeDtypeStruct((2 * SLOTS, 128), f32),
            jax.ShapeDtypeStruct((1, 128), f32),
        ),
        in_specs=[any_spec] * 9,
        out_specs=(vmem_spec,) * 3,
        scratch_shapes=scratch,
        compiler_params=pltpu.CompilerParams(
            collective_id=0, has_side_effects=True, vmem_limit_bytes=60 * 1024 * 1024
        ),
        cost_estimate=pl.CostEstimate(
            flops=3_500_000_000, bytes_accessed=12_000_000, transcendentals=0
        ),
    )(th, sh.T, pj, tq, tk, sq.T, sk.T, table, plan)
    return (
        hid.reshape(rows // 2),
        row.reshape(1, 1, SLOTS, HALF),
        loss[0, 0],
    )


def bit_groups(sizes):
    ny, nz, nx = sizes
    bx, bz, by = (n.bit_length() - 1 for n in (nx, nz, ny))
    return (
        tuple(range(bx)),
        tuple(range(bx, bx + bz)),
        tuple(range(bx + bz, bx + bz + by)),
    )


def solution(mesh, sizes=(4, 8, 4)):
    torus = Mesh(mesh.devices.reshape(*sizes, mesh.shape["head"]), DP_HEAD)
    placed = (
        P(DP, "head"),
        P(DP, None),
        P(None, "head"),
        P(DP, "head"),
        P(DP, "head"),
        P(DP, "head"),
        P(DP, "head"),
        P(),
        P(),
    )
    return jax.shard_map(
        functools.partial(body, sizes, bit_groups(sizes)),
        mesh=torus,
        in_specs=placed,
        out_specs=(P(DP_HEAD), P(DP, "head", None, None), P()),
        check_vma=False,
    )
```

time: 164 us -> 40 us (0.24)
  blocking collectives: 37.1 us -> 0 us
  local copies, waits for them, and re-layouts: 37.8 us -> 2.59 us
  Pallas kernels: 0 us -> 34.8 us
  starting transfers between devices: 32.9 us -> 0 us
  between operations: 20.9 us -> 2.4 us
  matrix products: 15.3 us -> 0 us
  other arithmetic: 14 us -> 0 us
  waiting for transfers between devices: 4.9 us -> 0 us
    psum x4 -> x0, blocking collectives: 37.1 us -> none  [one_axis_at_a_time(): return functools.reduce(lax.psum, axes, shard)]
    pallas_call x0 -> x1, Pallas kernels: none -> 34.8 us  [body(): pl.pallas_call(functools.partial(kernel, sizes, bits), name='distill', ou...]
    ppermute x7 -> x0, starting transfers between devices: 18.8 us -> none  [partner(): return lax.ppermute(value, axis, pairs)]
    another operation x11 -> x0, local copies, waits for them, and re-layouts: 16.2 us -> none
    dot_general x11 -> x0, matrix products: 15.3 us -> none  [the longest x5 6.17 us: branch(): jnp.einsum('ic,jc->ij', teach_query[:used_rows], teach_key[:used_rows], p...]
    all_to_all x2 -> x0, starting transfers between devices: 14.1 us -> none  [summed_on_arrival(): lax.all_to_all(blocks, axis, split_axis=0, concat_axis=0, tiled=True)]
    unnamed x18 -> x1, local copies, waits for them, and re-layouts: 14.3 us -> 1.29 us
    reduce_sum x7 -> x0, other arithmetic: 10.8 us -> none  [the longest x2 4.88 us: summed_on_arrival(): return arrived.sum(axis=0)]
  transfers between devices with their start and end apart: 9 -> 0, of which waited for: 1 -> 0; matrix products, arithmetic and copies ran while one was open for 6% -> 0% of each run, Pallas kernels for 0% -> 0%
where the time goes in v1:
time: 40 us; the launch traced here: 39.8 us
  Pallas kernels  34.8 us (87%)
  local copies, waits for them, and re-layouts  2.59 us (6%)
  between operations  2.4 us (6%)
    pallas_call x1, Pallas kernels, body(): pl.pallas_call(functools.partial(kernel, sizes, bits), name='distill', ou...  34.8 us
    reshape x1, local copies, waits for them, and re-layouts, body(): return (hid.reshape(rows // 2), row.reshape(1, 1, SLOTS, HALF), loss[0, 0])  1.3 us
    unnamed x1, local copies, waits for them, and re-layouts  1.29 us

profile of v1, /device:TPU:1, one launch (start us, length us, event | category | flops | bytes accessed | tf_op | source)
XLA Modules:
  0.0 39.8 jit_solution(6194061496824061938)
XLA Ops:
  0.6 34.8 %distill.1 = (f32[10,128]{1,0:T(8,128)}, f32[10,128]{1,0:T(8,128)}, f32[1,128]{1,0:T(1,128)}) custom-call(bf16[2560,512]{1,0:T(8,128)(2,1)} %th.1, bf16[312,2560]{1,0:T(8,128)(2,1)} %bitcast.8, bf16[312,512]{1,0:T(8,128)(2,1)} %pj.1, bf16[2560,512]{1,0:T(8,128)(2,1)} %tq.1, bf16[2560,512]{1,0:T(8,128)(2,1)} %tk.1, bf16[156,2560]{1,0:T(8,128)(2,1)} %bitcast.9, ...), custom_call_target="tpu_custom_call" | custom-call | flops 3500000000 | bytes 12000000 | tf_op jit(solution)/shard_map/distill/pallas_call | solution.py:411
  35.4 1.3 %reshape.18 = f32[1,1,5,256]{3,1,2,0:T(1,128)} reshape(f32[10,128]{1,0:T(8,128)} %get-tuple-element.7) | data formatting | bytes 10240 | tf_op jit(solution)/shard_map/reshape | solution.py:431
  36.7 1.3 %copy.16 = f32[1280]{0:T(1024)} copy(f32[1280]{0:T(1024)} %bitcast.7) | data formatting | bytes 10240

commit v2 on v1

v2 whole, which is shorter than its diff:
```python
import functools
import math

import jax
import jax.numpy as jnp
from jax import lax
from jax.experimental import pallas as pl
from jax.experimental.pallas import tpu as pltpu
from jax.sharding import Mesh
from jax.sharding import PartitionSpec as P

HEADS_T = 16
HEAD_T = 64
HEADS_S = 12
HEAD_S = 26
MAXLEN = 512
HALF = 256
SLOTS = 5
D_T = 1024
DP = ("dp_0", "dp_1", "dp_2")
DP_HEAD = ("dp_0", "dp_1", "dp_2", "head")
MESH = pl.DeviceIdType.MESH

T_SCALE = 1.0 / (HEADS_T * math.sqrt(HEAD_T))
S_SCALE = 1.0 / (HEADS_S * math.sqrt(HEAD_S))
KAPPA = S_SCALE / T_SCALE
OUT_SCALE = T_SCALE * T_SCALE


def flip(device, bit):
    mask = 2**bit
    return device + mask * (1 - 2 * ((device // mask) % 2))


def trace_forward(plan, device, slot, bits):
    for bit in bits:
        other = flip(device, bit)
        moves = plan[bit, device] == slot
        slot = jnp.where(moves, plan[bit, other], slot)
        device = jnp.where(moves, other, device)
    return device, slot


def trace_backward(plan, device, slot, bits):
    return trace_forward(plan, device, slot, tuple(reversed(bits)))


def kernel(
    sizes,
    bits,
    th,
    sht,
    pj,
    tq,
    tk,
    sqt,
    skt,
    lens,
    plan,
    hid_out,
    row_out,
    loss_out,
    tk_v,
    tq_v,
    sk_v,
    sq_v,
    th_v,
    sh_v,
    pj_v,
    len_v,
    len_s,
    plan_s,
    map_send,
    map_own,
    map_recv,
    hid_send,
    hid_recv,
    send_a,
    send_b,
    recv_a,
    recv_b,
    cross_b,
    rows_a,
    rows_b,
    load_sem,
    small_sem,
    map_ssem,
    map_rsem,
    hid_sem,
    ssem_a,
    rsem_a,
    ssem_b,
    rsem_b,
    ssem_c,
    rsem_c,
):
    ny, nz, nx = sizes
    y, z, x = (lax.axis_index(name) for name in DP)
    head = lax.axis_index("head")
    away = 1 - head
    plane = nz * nx
    spot = z * nx + x
    me = y * plane + spot

    small = [
        pltpu.make_async_copy(plan, plan_s, small_sem.at[0]),
        pltpu.make_async_copy(lens, len_s, small_sem.at[1]),
        pltpu.make_async_copy(lens, len_v, small_sem.at[2]),
    ]
    loads = []
    for s in range(SLOTS):
        n = 6 * s
        copies = [
            pltpu.make_async_copy(tk.at[pl.ds(s * MAXLEN, MAXLEN)], tk_v.at[s], load_sem.at[n]),
            pltpu.make_async_copy(
                skt.at[:, pl.ds(s * MAXLEN, MAXLEN)], sk_v.at[s], load_sem.at[n + 1]
            ),
        ]
        for h, half in enumerate((away, head)):
            first = pl.multiple_of(s * MAXLEN + half * HALF, HALF)
            place = pl.ds(h * HALF, HALF)
            copies += [
                pltpu.make_async_copy(
                    tq.at[pl.ds(first, HALF)], tq_v.at[s, place], load_sem.at[n + 2 + 2 * h]
                ),
                pltpu.make_async_copy(
                    sqt.at[:, pl.ds(first, HALF)], sq_v.at[s, :, place], load_sem.at[n + 3 + 2 * h]
                ),
            ]
        loads.append(copies)
    base = 6 * SLOTS
    load_pj = pltpu.make_async_copy(pj, pj_v, load_sem.at[base])
    hid_loads = []
    for b in range(2 * SLOTS):
        half = away if b < SLOTS else head
        first = pl.multiple_of((half * SLOTS + b % SLOTS) * HALF, HALF)
        n = base + 1 + 2 * b
        hid_loads.append(
            [
                pltpu.make_async_copy(sht.at[:, pl.ds(first, HALF)], sh_v.at[b], load_sem.at[n]),
                pltpu.make_async_copy(th.at[pl.ds(first, HALF)], th_v.at[b], load_sem.at[n + 1]),
            ]
        )
    for copy in loads[0] + small:
        copy.start()

    offsets = [(dz, dx) for dz in range(nz) for dx in range(nx) if dz or dx]
    offsets.sort(key=lambda o: -min(o[0], nz - o[0]) - min(o[1], nx - o[1]))
    targets_a = [((z + dz) % nz, (x + dx) % nx) for dz, dx in offsets]
    peers = [{"head": away}]
    peers += [{"dp_1": tz, "dp_2": tx} for tz, tx in targets_a]
    peers += [{"dp_0": (y + k) % ny} for k in range(1, ny)]
    peers += [{"dp_0": (y + k) % ny, "head": away} for k in range(1, ny)]
    barrier = pltpu.get_barrier_semaphore()
    for copy in loads[1]:
        copy.start()
    for peer in peers:
        pl.semaphore_signal(barrier, inc=1, device_id=peer, device_id_type=MESH)
    for copy in loads[2]:
        copy.start()

    ahead = {0: loads[3], 1: loads[4], 2: [load_pj] + hid_loads[0] + hid_loads[1]}
    ahead[3] = hid_loads[2] + hid_loads[3] + hid_loads[4]
    ahead[4] = hid_loads[5] + hid_loads[6]
    later = {g: hid_loads[g + 7] for g in range(3)}

    def length_of(slot):
        index = me * SLOTS + slot
        return len_s[index // 128, index % 128]

    def routes():
        lands = [trace_forward(plan_s, me, s, bits[0])[0] for s in range(SLOTS)]
        gives_a = []
        for tz, tx in targets_a:
            target = y * plane + tz * nx + tx
            slot = jnp.int32(0)
            for s in range(1, SLOTS):
                slot = jnp.where(lands[s] == target, s, slot)
            gives_a.append(slot)
        lands = [trace_forward(plan_s, me, s, bits[1])[0] for s in range(SLOTS)]
        gives_b = []
        for k in range(1, ny):
            target = ((y + k) % ny) * plane + spot
            slot = jnp.int32(0)
            for s in range(1, SLOTS):
                slot = jnp.where(lands[s] == target, s, slot)
            gives_b.append(slot)
        takes = []
        for rounds, stride, count in ((bits[0], 1, plane), (bits[1], plane, ny)):
            take = []
            for s in range(SLOTS):
                device, slot = trace_backward(plan_s, me, s, rounds)
                source = (device // stride) % count
                take.append(jnp.where(device == me, 2 * count + slot, 2 * source))
            takes.append(take)
        return gives_a, gives_b, takes[0], takes[1]

    map_copies = []
    for s in range(SLOTS):
        for copy in loads[s]:
            copy.wait()
        if s == 0:
            for copy in small:
                copy.wait()
        for copy in ahead[s]:
            copy.start()
        teacher = lax.dot_general(
            tk_v[s], tq_v[s], (((1,), (1,)), ((), ())), preferred_element_type=jnp.float32
        )
        student = lax.dot_general(
            sk_v[s], sq_v[s], (((0,), (0,)), ((), ())), preferred_element_type=jnp.float32
        )
        partial = teacher - KAPPA * student
        map_send[s] = partial[:, :HALF]
        map_own[s] = partial[:, HALF:]
        if s == 0:
            gives_a, gives_b, takes_a, takes_b = routes()
            pl.semaphore_wait(barrier, len(peers))
        copy = pltpu.make_async_remote_copy(
            src_ref=map_send.at[s],
            dst_ref=map_recv.at[s],
            send_sem=map_ssem.at[s],
            recv_sem=map_rsem.at[s],
            device_id={"head": away},
            device_id_type=MESH,
        )
        copy.start()
        map_copies.append(copy)

    lane = lax.broadcasted_iota(jnp.int32, (1, HALF), 1)
    sublane = lax.broadcasted_iota(jnp.int32, (8, HALF), 0)

    def hidden_block(b):
        projected = lax.dot_general(
            sh_v[b], pj_v[...], (((0,), (0,)), ((), ())), preferred_element_type=jnp.float32
        )
        errors = projected - th_v[b].astype(jnp.float32)
        squares = errors * errors
        folded = squares[:, :128]
        for c in range(128, squares.shape[1], 128):
            folded = folded + squares[:, c : c + 128]
        sums = jnp.sum(folded.T, axis=0, keepdims=True)
        half = away if b < SLOTS else head
        block = half * SLOTS + b % SLOTS
        inside = lane + (block % 2) * HALF < length_of(block // 2)
        return jnp.where(inside, sums, 0.0)

    def row_sums(s):
        length = length_of(s)
        accs = [jnp.zeros((8, HALF), jnp.float32) for _ in range(4)]
        for r in range(MAXLEN // 8):
            part = map_own[s, 8 * r : 8 * r + 8, :] + map_recv[s, 8 * r : 8 * r + 8, :]
            part = jnp.where(sublane < length - 8 * r, part, 0.0)
            accs[r % 4] = accs[r % 4] + part * part
        acc = (accs[0] + accs[1]) + (accs[2] + accs[3])
        sums = jnp.sum(acc, axis=0, keepdims=True) * OUT_SCALE
        sums = jnp.where(lane + head * HALF < length, sums, 0.0)
        rows_a[s] = sums / length.astype(jnp.float32)
        return sums

    own_hidden = []
    attention = jnp.zeros((1, HALF), jnp.float32)
    load_pj.wait()
    for g in range(SLOTS):
        for b in (2 * g, 2 * g + 1):
            for copy in hid_loads[b]:
                copy.wait()
        for copy in later.get(g, ()):
            copy.start()
        map_copies[g].wait_recv()
        for b in (2 * g, 2 * g + 1):
            sums = hidden_block(b)
            if b < SLOTS:
                hid_send[b] = sums
            else:
                own_hidden.append(sums)
        attention = attention + row_sums(g)
        if 2 * g <= SLOTS - 1 <= 2 * g + 1:
            hid_copy = pltpu.make_async_remote_copy(
                src_ref=hid_send,
                dst_ref=hid_recv,
                send_sem=hid_sem.at[0],
                recv_sem=hid_sem.at[1],
                device_id={"head": away},
                device_id_type=MESH,
            )
            hid_copy.start()

    hid_copy.wait_recv()
    hidden = jnp.zeros((1, HALF), jnp.float32)
    for b in range(SLOTS):
        total = (own_hidden[b] + hid_recv[b]) * (1.0 / D_T)
        hid_out[2 * b : 2 * b + 1, :] = total[:, :128]
        hid_out[2 * b + 1 : 2 * b + 2, :] = total[:, 128:]
        hidden = hidden + total

    totals = jnp.concatenate(
        [hidden[:, :128] + hidden[:, 128:], attention[:, :128] + attention[:, 128:]], axis=1
    )

    def exchange(peers, slot, count, totals, rows, buffer, send, ssem, rsem, give):
        copies = []
        for k, peer in enumerate(peers):
            send[2 * k] = rows[give[k]]
            send[2 * k + 1] = totals
            copies.append(
                pltpu.make_async_remote_copy(
                    src_ref=send.at[pl.ds(2 * k, 2)],
                    dst_ref=buffer.at[pl.ds(2 * slot, 2)],
                    send_sem=ssem.at[k],
                    recv_sem=rsem.at[k],
                    device_id=peer,
                    device_id_type=MESH,
                )
            )
            copies[-1].start()
        buffer[2 * slot + 1] = totals
        for s in range(SLOTS):
            buffer[2 * count + s] = rows[s]
        return copies

    def summed(rows):
        while len(rows) > 1:
            rows = [functools.reduce(lambda a, b: a + b, rows[i : i + 2]) for i in range(0, len(rows), 2)]
        return rows[0]

    a_peers = [{"dp_1": tz, "dp_2": tx} for tz, tx in targets_a]
    a_copies = exchange(a_peers, spot, plane, totals, rows_a, recv_a, send_a, ssem_a, rsem_a, gives_a)
    counted = len_v[...].astype(jnp.float32)
    tokens = jnp.sum(jnp.sum(counted, axis=0, keepdims=True), axis=1, keepdims=True)
    pairs = jnp.sum(jnp.sum(counted * counted, axis=0, keepdims=True), axis=1, keepdims=True)
    for copy in a_copies:
        copy.wait_recv()
    for s in range(SLOTS):
        rows_b[s] = recv_a[takes_a[s]]
    totals = summed([recv_a[2 * i + 1] for i in range(plane)])

    b_peers = [{"dp_0": (y + k) % ny} for k in range(1, ny)]
    b_copies = exchange(b_peers, y, ny, totals, rows_b, recv_b, send_b, ssem_b, rsem_b, gives_b)
    crosses = []
    for k in range(ny):
        copy = pltpu.make_async_remote_copy(
            src_ref=send_b.at[pl.ds(1, 1)],
            dst_ref=cross_b.at[pl.ds(y, 1)],
            send_sem=ssem_c.at[k],
            recv_sem=rsem_c.at[k],
            device_id={"dp_0": (y + k) % ny, "head": away},
            device_id_type=MESH,
        )
        copy.start()
        crosses.append(copy)
    for copy in map_copies + [hid_copy] + a_copies:
        copy.wait_send()
    for copy in b_copies:
        copy.wait_recv()
    for s in range(SLOTS):
        row_out[s] = recv_b[takes_b[s]]
    for copy in crosses:
        copy.wait_recv()
    same = summed([recv_b[2 * i + 1] for i in range(ny)])
    cross = summed([cross_b[i] for i in range(ny)])
    totals = same + cross
    hidden_total = jnp.sum(totals[:, :128], axis=1, keepdims=True)
    attention_total = jnp.sum(totals[:, 128:], axis=1, keepdims=True)
    loss = hidden_total / tokens + attention_total / pairs
    loss_out[...] = jnp.broadcast_to(loss, loss_out.shape)

    for copy in b_copies + crosses:
        copy.wait_send()


def deliver(*refs):
    sources, targets, sem = refs[:3], refs[3:6], refs[6]
    copies = [
        pltpu.make_async_copy(source, target, sem.at[n])
        for n, (source, target) in enumerate(zip(sources, targets))
    ]
    for copy in copies:
        copy.start()
    for copy in copies:
        copy.wait()


def body(sizes, bits, th, sh, pj, tq, tk, sq, sk, lengths, plan):
    ny, nz, nx = sizes
    rows = th.shape[0]
    d_s = sh.shape[1]
    half_t, half_s = tq.shape[1], sq.shape[1]
    bf16, f32 = jnp.bfloat16, jnp.float32
    table = lengths.reshape(-1, 128)
    any_spec = pl.BlockSpec(memory_space=pl.ANY)
    vmem_spec = pl.BlockSpec(memory_space=pltpu.VMEM)
    dma = pltpu.SemaphoreType.DMA
    plane = nz * nx
    scratch = [
        pltpu.VMEM((SLOTS, MAXLEN, half_t), bf16),
        pltpu.VMEM((SLOTS, MAXLEN, half_t), bf16),
        pltpu.VMEM((SLOTS, half_s, MAXLEN), bf16),
        pltpu.VMEM((SLOTS, half_s, MAXLEN), bf16),
        pltpu.VMEM((2 * SLOTS, HALF, half_t), bf16),
        pltpu.VMEM((2 * SLOTS, d_s, HALF), bf16),
        pltpu.VMEM((d_s, half_t), bf16),
        pltpu.VMEM(table.shape, jnp.int32),
        pltpu.SMEM(table.shape, jnp.int32),
        pltpu.SMEM(plan.shape, jnp.int32),
        pltpu.VMEM((SLOTS, MAXLEN, HALF), f32),
        pltpu.VMEM((SLOTS, MAXLEN, HALF), f32),
        pltpu.VMEM((SLOTS, MAXLEN, HALF), f32),
        pltpu.VMEM((SLOTS, 1, HALF), f32),
        pltpu.VMEM((SLOTS, 1, HALF), f32),
        pltpu.VMEM((2 * (plane - 1), 1, HALF), f32),
        pltpu.VMEM((2 * (ny - 1), 1, HALF), f32),
        pltpu.VMEM((2 * plane + SLOTS, 1, HALF), f32),
        pltpu.VMEM((2 * ny + SLOTS, 1, HALF), f32),
        pltpu.VMEM((ny, 1, HALF), f32),
        pltpu.VMEM((SLOTS, 1, HALF), f32),
        pltpu.VMEM((SLOTS, 1, HALF), f32),
        dma((6 * SLOTS + 1 + 4 * SLOTS,)),
        dma((3,)),
        dma((SLOTS,)),
        dma((SLOTS,)),
        dma((2,)),
        dma((plane - 1,)),
        dma((plane - 1,)),
        dma((ny - 1,)),
        dma((ny - 1,)),
        dma((ny,)),
        dma((ny,)),
    ]
    shapes = ((2 * SLOTS, 128), (SLOTS, 1, HALF), (1, 128))
    results = pl.pallas_call(
        functools.partial(kernel, sizes, bits),
        name="distill",
        out_shape=tuple(pltpu.VMEM(shape, f32) for shape in shapes),
        in_specs=[any_spec] * 9,
        out_specs=(vmem_spec,) * 3,
        scratch_shapes=scratch,
        compiler_params=pltpu.CompilerParams(
            collective_id=0, has_side_effects=True, vmem_limit_bytes=60 * 1024 * 1024
        ),
        cost_estimate=pl.CostEstimate(
            flops=3_500_000_000, bytes_accessed=12_000_000, transcendentals=0
        ),
    )(th, sh.T, pj, tq, tk, sq.T, sk.T, table, plan)
    hid, row, loss = pl.pallas_call(
        deliver,
        name="deliver",
        out_shape=tuple(jax.ShapeDtypeStruct(shape, f32) for shape in shapes),
        in_specs=[vmem_spec] * 3,
        out_specs=(any_spec,) * 3,
        scratch_shapes=[dma((3,))],
    )(*(pltpu.with_memory_space_constraint(result, pltpu.VMEM) for result in results))
    return (
        hid.reshape(rows // 2),
        row.reshape(1, 1, SLOTS, HALF),
        loss[0, 0],
    )


def bit_groups(sizes):
    ny, nz, nx = sizes
    first = (nx * nz).bit_length() - 1
    return tuple(range(first)), tuple(range(first, first + ny.bit_length() - 1))


def solution(mesh, sizes=(4, 8, 4)):
    torus = Mesh(mesh.devices.reshape(*sizes, mesh.shape["head"]), DP_HEAD)
    placed = (
        P(DP, "head"),
        P(DP, None),
        P(None, "head"),
        P(DP, "head"),
        P(DP, "head"),
        P(DP, "head"),
        P(DP, "head"),
        P(),
        P(),
    )
    return jax.shard_map(
        functools.partial(body, sizes, bit_groups(sizes)),
        mesh=torus,
        in_specs=placed,
        out_specs=(P(DP_HEAD), P(DP, "head", None, None), P()),
        check_vma=False,
    )
```

time: 40 us -> 28.6 us (0.72)
  Pallas kernels: 34.8 us -> 27.8 us
  local copies, waits for them, and re-layouts: 2.59 us -> 0 us
  between operations: 2.4 us -> 0.64 us
    pallas_call x1, Pallas kernels: 34.8 us -> 27.2 us  [body(): pl.pallas_call(functools.partial(kernel, sizes, bits), name='distill', ou...]
    reshape x1 -> x0, local copies, waits for them, and re-layouts: 1.3 us -> none  [body(): return (hid.reshape(rows // 2), row.reshape(1, 1, SLOTS, HALF), loss[0, 0])]
    unnamed x1 -> x0, local copies, waits for them, and re-layouts: 1.29 us -> none
    pallas_call x0 -> x1, Pallas kernels: none -> 0.63 us  [body(): pl.pallas_call(deliver, name='deliver', out_shape=tuple((jax.ShapeDtypeSt...]
where the time goes in v2:
time: 28.6 us; the launch traced here: 28.5 us
  Pallas kernels  27.8 us (97%)
  between operations  0.64 us (2%)
    pallas_call x1, Pallas kernels, body(): pl.pallas_call(functools.partial(kernel, sizes, bits), name='distill', ou...  27.2 us
    pallas_call x1, Pallas kernels, body(): pl.pallas_call(deliver, name='deliver', out_shape=tuple((jax.ShapeDtypeSt...  0.63 us

profile of v2, /device:TPU:1, one launch (start us, length us, event | category | flops | bytes accessed | tf_op | source)
XLA Modules:
  0.0 28.5 jit_solution(16560435826545965769)
XLA Ops:
  0.6 27.2 %distill.1 = (f32[10,128]{1,0:T(8,128)S(1)}, f32[5,1,256]{2,1,0:T(1,128)S(1)}, f32[1,128]{1,0:T(1,128)S(1)}) custom-call(bf16[2560,512]{1,0:T(8,128)(2,1)} %th.1, bf16[312,2560]{1,0:T(8,128)(2,1)} %bitcast.10, bf16[312,512]{1,0:T(8,128)(2,1)} %pj.1, bf16[2560,512]{1,0:T(8,128)(2,1)} %tq.1, bf16[2560,512]{1,0:T(8,128)(2,1)} %tk.1, ...), custom_call_target="tpu_custom_call" | custom-call | flops 3500000000 | bytes 12000000 | tf_op jit(solution)/shard_map/distill/pallas_call | solution.py:431
  27.9 0.6 %deliver.1 = (f32[10,128]{1,0:T(8,128)}, f32[5,1,256]{2,1,0:T(1,128)}, f32[1,128]{1,0:T(1,128)}) custom-call(f32[10,128]{1,0:T(8,128)S(1)} %get-tuple-element.9.refs_0_, f32[5,1,256]{2,1,0:T(1,128)S(1)} %get-tuple-element.10.refs_1_, f32[1,128]{1,0:T(1,128)S(1)} %get-tuple-element.11.refs_2_), custom_call_target="tpu_custom_call" | custom-call | tf_op jit(solution)/shard_map/deliver/pallas_call | solution.py:445

commit v3 on v2

--- a/solution.py
+++ b/solution.py
@@ -28,8 +28,7 @@
 
 
 def flip(device, bit):
-    mask = 2**bit
-    return device + mask * (1 - 2 * ((device // mask) % 2))
+    return lax.bitwise_xor(device, jnp.int32(2**bit))
 
 
 def trace_forward(plan, device, slot, bits):
@@ -93,6 +92,7 @@
     rsem_b,
     ssem_c,
     rsem_c,
+    greet_sem,
 ):
     ny, nz, nx = sizes
     y, z, x = (lax.axis_index(name) for name in DP)
@@ -141,21 +141,34 @@
                 pltpu.make_async_copy(th.at[pl.ds(first, HALF)], th_v.at[b], load_sem.at[n + 1]),
             ]
         )
-    for copy in loads[0] + small:
+    for copy in small[:2] + loads[0] + small[2:]:
         copy.start()
 
     offsets = [(dz, dx) for dz in range(nz) for dx in range(nx) if dz or dx]
     offsets.sort(key=lambda o: -min(o[0], nz - o[0]) - min(o[1], nx - o[1]))
     targets_a = [((z + dz) % nz, (x + dx) % nx) for dz, dx in offsets]
-    peers = [{"head": away}]
-    peers += [{"dp_1": tz, "dp_2": tx} for tz, tx in targets_a]
-    peers += [{"dp_0": (y + k) % ny} for k in range(1, ny)]
-    peers += [{"dp_0": (y + k) % ny, "head": away} for k in range(1, ny)]
+    chips = [{"dp_1": tz, "dp_2": tx, "head": 1} for tz, tx in targets_a]
+    chips += [{"dp_0": (y + k) % ny, "head": 1} for k in range(1, ny)]
     barrier = pltpu.get_barrier_semaphore()
+
+    @pl.when(head == 1)
+    def _():
+        pl.semaphore_signal(barrier, inc=1, device_id={"head": 0}, device_id_type=MESH)
+
     for copy in loads[1]:
         copy.start()
-    for peer in peers:
-        pl.semaphore_signal(barrier, inc=1, device_id=peer, device_id_type=MESH)
+
+    @pl.when(head == 0)
+    def _():
+        pl.semaphore_wait(barrier, 1)
+        pl.semaphore_signal(greet_sem.at[0], inc=1, device_id={"head": 1}, device_id_type=MESH)
+
+    @pl.when(head == 1)
+    def _():
+        pl.semaphore_wait(greet_sem.at[0], 1)
+        for chip in chips:
+            pl.semaphore_signal(barrier, inc=1, device_id=chip, device_id_type=MESH)
+
     for copy in loads[2]:
         copy.start()
 
@@ -190,18 +203,21 @@
             take = []
             for s in range(SLOTS):
                 device, slot = trace_backward(plan_s, me, s, rounds)
-                source = (device // stride) % count
+                source = lax.bitwise_and(
+                    lax.shift_right_logical(device, jnp.int32(stride.bit_length() - 1)),
+                    jnp.int32(count - 1),
+                )
                 take.append(jnp.where(device == me, 2 * count + slot, 2 * source))
             takes.append(take)
         return gives_a, gives_b, takes[0], takes[1]
 
+    for copy in small:
+        copy.wait()
+    gives_a, gives_b, takes_a, takes_b = routes()
     map_copies = []
     for s in range(SLOTS):
         for copy in loads[s]:
             copy.wait()
-        if s == 0:
-            for copy in small:
-                copy.wait()
         for copy in ahead[s]:
             copy.start()
         teacher = lax.dot_general(
@@ -213,9 +229,6 @@
         partial = teacher - KAPPA * student
         map_send[s] = partial[:, :HALF]
         map_own[s] = partial[:, HALF:]
-        if s == 0:
-            gives_a, gives_b, takes_a, takes_b = routes()
-            pl.semaphore_wait(barrier, len(peers))
         copy = pltpu.make_async_remote_copy(
             src_ref=map_send.at[s],
             dst_ref=map_recv.at[s],
@@ -323,6 +336,15 @@
         while len(rows) > 1:
             rows = [functools.reduce(lambda a, b: a + b, rows[i : i + 2]) for i in range(0, len(rows), 2)]
         return rows[0]
+
+    @pl.when(head == 1)
+    def _():
+        pl.semaphore_wait(barrier, len(chips))
+        pl.semaphore_signal(greet_sem.at[1], inc=1, device_id={"head": 0}, device_id_type=MESH)
+
+    @pl.when(head == 0)
+    def _():
+        pl.semaphore_wait(greet_sem.at[1], 1)
 
     a_peers = [{"dp_1": tz, "dp_2": tx} for tz, tx in targets_a]
     a_copies = exchange(a_peers, spot, plane, totals, rows_a, recv_a, send_a, ssem_a, rsem_a, gives_a)
@@ -426,6 +448,7 @@
         dma((ny - 1,)),
         dma((ny,)),
         dma((ny,)),
+        pltpu.SemaphoreType.REGULAR((2,)),
     ]
     shapes = ((2 * SLOTS, 128), (SLOTS, 1, HALF), (1, 128))
     results = pl.pallas_call(

time: 28.6 us -> 27.4 us (0.958)
  Pallas kernels: 27.8 us -> 26.7 us
    pallas_call x1, Pallas kernels: 27.2 us -> 26.1 us  [body(): pl.pallas_call(functools.partial(kernel, sizes, bits), name='distill', ou...]
where the time goes in v3:
time: 27.4 us; the launch traced here: 27.3 us
  Pallas kernels  26.7 us (97%)
  between operations  0.64 us (2%)
    pallas_call x1, Pallas kernels, body(): pl.pallas_call(functools.partial(kernel, sizes, bits), name='distill', ou...  26.1 us
    pallas_call x1, Pallas kernels, body(): pl.pallas_call(deliver, name='deliver', out_shape=tuple((jax.ShapeDtypeSt...  0.63 us

profile of v3, /device:TPU:1, one launch (start us, length us, event | category | flops | bytes accessed | tf_op | source)
XLA Modules:
  0.0 27.3 jit_solution(13164546952681446615)
XLA Ops:
  0.6 26.1 %distill.1 = (f32[10,128]{1,0:T(8,128)S(1)}, f32[5,1,256]{2,1,0:T(1,128)S(1)}, f32[1,128]{1,0:T(1,128)S(1)}) custom-call(bf16[2560,512]{1,0:T(8,128)(2,1)} %th.1, bf16[312,2560]{1,0:T(8,128)(2,1)} %bitcast.10, bf16[312,512]{1,0:T(8,128)(2,1)} %pj.1, bf16[2560,512]{1,0:T(8,128)(2,1)} %tq.1, bf16[2560,512]{1,0:T(8,128)(2,1)} %tk.1, ...), custom_call_target="tpu_custom_call" | custom-call | flops 3500000000 | bytes 12000000 | tf_op jit(solution)/shard_map/distill/pallas_call | solution.py:454
  26.7 0.6 %deliver.1 = (f32[10,128]{1,0:T(8,128)}, f32[5,1,256]{2,1,0:T(1,128)}, f32[1,128]{1,0:T(1,128)}) custom-call(f32[10,128]{1,0:T(8,128)S(1)} %get-tuple-element.9.refs_0_, f32[5,1,256]{2,1,0:T(1,128)S(1)} %get-tuple-element.10.refs_1_, f32[1,128]{1,0:T(1,128)S(1)} %get-tuple-element.11.refs_2_), custom_call_target="tpu_custom_call" | custom-call | tf_op jit(solution)/shard_map/deliver/pallas_call | solution.py:468

commit v4 on v3

--- a/solution.py
+++ b/solution.py
@@ -78,9 +78,9 @@
     send_b,
     recv_a,
     recv_b,
-    cross_b,
     rows_a,
     rows_b,
+    rows_c,
     load_sem,
     small_sem,
     map_ssem,
@@ -90,8 +90,7 @@
     rsem_a,
     ssem_b,
     rsem_b,
-    ssem_c,
-    rsem_c,
+    own_sem,
     greet_sem,
 ):
     ny, nz, nx = sizes
@@ -155,9 +154,6 @@
     def _():
         pl.semaphore_signal(barrier, inc=1, device_id={"head": 0}, device_id_type=MESH)
 
-    for copy in loads[1]:
-        copy.start()
-
     @pl.when(head == 0)
     def _():
         pl.semaphore_wait(barrier, 1)
@@ -168,18 +164,6 @@
         pl.semaphore_wait(greet_sem.at[0], 1)
         for chip in chips:
             pl.semaphore_signal(barrier, inc=1, device_id=chip, device_id_type=MESH)
-
-    for copy in loads[2]:
-        copy.start()
-
-    ahead = {0: loads[3], 1: loads[4], 2: [load_pj] + hid_loads[0] + hid_loads[1]}
-    ahead[3] = hid_loads[2] + hid_loads[3] + hid_loads[4]
-    ahead[4] = hid_loads[5] + hid_loads[6]
-    later = {g: hid_loads[g + 7] for g in range(3)}
-
-    def length_of(slot):
-        index = me * SLOTS + slot
-        return len_s[index // 128, index % 128]
 
     def routes():
         lands = [trace_forward(plan_s, me, s, bits[0])[0] for s in range(SLOTS)]
@@ -211,34 +195,53 @@
             takes.append(take)
         return gives_a, gives_b, takes[0], takes[1]
 
+    for copy in loads[1]:
+        copy.start()
     for copy in small:
         copy.wait()
+    for copy in loads[2]:
+        copy.start()
     gives_a, gives_b, takes_a, takes_b = routes()
+    for copy in loads[3]:
+        copy.start()
+
+    ahead = {
+        0: loads[4] + [load_pj] + hid_loads[0] + hid_loads[1],
+        1: sum(hid_loads[2:6], []),
+        3: sum(hid_loads[6:], []),
+    }
+
+    def length_of(slot):
+        index = me * SLOTS + slot
+        return len_s[index // 128, index % 128]
+
     map_copies = []
-    for s in range(SLOTS):
-        for copy in loads[s]:
-            copy.wait()
-        for copy in ahead[s]:
+    for group in ((0,), (1, 2), (3, 4)):
+        for s in group:
+            for copy in loads[s]:
+                copy.wait()
+        for copy in ahead[group[0]]:
             copy.start()
-        teacher = lax.dot_general(
-            tk_v[s], tq_v[s], (((1,), (1,)), ((), ())), preferred_element_type=jnp.float32
-        )
-        student = lax.dot_general(
-            sk_v[s], sq_v[s], (((0,), (0,)), ((), ())), preferred_element_type=jnp.float32
-        )
-        partial = teacher - KAPPA * student
-        map_send[s] = partial[:, :HALF]
-        map_own[s] = partial[:, HALF:]
-        copy = pltpu.make_async_remote_copy(
-            src_ref=map_send.at[s],
-            dst_ref=map_recv.at[s],
-            send_sem=map_ssem.at[s],
-            recv_sem=map_rsem.at[s],
-            device_id={"head": away},
-            device_id_type=MESH,
-        )
-        copy.start()
-        map_copies.append(copy)
+        for s in group:
+            teacher = lax.dot_general(
+                tk_v[s], tq_v[s], (((1,), (1,)), ((), ())), preferred_element_type=jnp.float32
+            )
+            student = lax.dot_general(
+                sk_v[s], sq_v[s], (((0,), (0,)), ((), ())), preferred_element_type=jnp.float32
+            )
+            partial = teacher - KAPPA * student
+            map_send[s] = partial[:, :HALF]
+            map_own[s] = partial[:, HALF:]
+            copy = pltpu.make_async_remote_copy(
+                src_ref=map_send.at[s],
+                dst_ref=map_recv.at[s],
+                send_sem=map_ssem.at[s],
+                recv_sem=map_rsem.at[s],
+                device_id={"head": away},
+                device_id_type=MESH,
+            )
+            copy.start()
+            map_copies.append(copy)
 
     lane = lax.broadcasted_iota(jnp.int32, (1, HALF), 1)
     sublane = lax.broadcasted_iota(jnp.int32, (8, HALF), 0)
@@ -271,33 +274,31 @@
         rows_a[s] = sums / length.astype(jnp.float32)
         return sums
 
-    own_hidden = []
+    hid_copy = pltpu.make_async_remote_copy(
+        src_ref=hid_send,
+        dst_ref=hid_recv,
+        send_sem=hid_sem.at[0],
+        recv_sem=hid_sem.at[1],
+        device_id={"head": away},
+        device_id_type=MESH,
+    )
     attention = jnp.zeros((1, HALF), jnp.float32)
     load_pj.wait()
-    for g in range(SLOTS):
-        for b in (2 * g, 2 * g + 1):
+    for g in range(2):
+        blocks = range(SLOTS * g, SLOTS * (g + 1))
+        for b in blocks:
             for copy in hid_loads[b]:
                 copy.wait()
-        for copy in later.get(g, ()):
-            copy.start()
         map_copies[g].wait_recv()
-        for b in (2 * g, 2 * g + 1):
-            sums = hidden_block(b)
-            if b < SLOTS:
-                hid_send[b] = sums
-            else:
-                own_hidden.append(sums)
+        own_hidden = [hidden_block(b) for b in blocks]
         attention = attention + row_sums(g)
-        if 2 * g <= SLOTS - 1 <= 2 * g + 1:
-            hid_copy = pltpu.make_async_remote_copy(
-                src_ref=hid_send,
-                dst_ref=hid_recv,
-                send_sem=hid_sem.at[0],
-                recv_sem=hid_sem.at[1],
-                device_id={"head": away},
-                device_id_type=MESH,
-            )
+        if g == 0:
+            for b in blocks:
+                hid_send[b] = own_hidden[b]
             hid_copy.start()
+    for s in range(2, SLOTS):
+        map_copies[s].wait_recv()
+        attention = attention + row_sums(s)
 
     hid_copy.wait_recv()
     hidden = jnp.zeros((1, HALF), jnp.float32)
@@ -311,84 +312,132 @@
         [hidden[:, :128] + hidden[:, 128:], attention[:, :128] + attention[:, 128:]], axis=1
     )
 
-    def exchange(peers, slot, count, totals, rows, buffer, send, ssem, rsem, give):
-        copies = []
-        for k, peer in enumerate(peers):
-            send[2 * k] = rows[give[k]]
-            send[2 * k + 1] = totals
-            copies.append(
-                pltpu.make_async_remote_copy(
-                    src_ref=send.at[pl.ds(2 * k, 2)],
-                    dst_ref=buffer.at[pl.ds(2 * slot, 2)],
-                    send_sem=ssem.at[k],
-                    recv_sem=rsem.at[k],
-                    device_id=peer,
-                    device_id_type=MESH,
-                )
-            )
-            copies[-1].start()
-        buffer[2 * slot + 1] = totals
-        for s in range(SLOTS):
-            buffer[2 * count + s] = rows[s]
-        return copies
+    @pl.when(head == 1)
+    def _():
+        pl.semaphore_wait(barrier, len(chips))
+        pl.semaphore_signal(greet_sem.at[1], inc=1, device_id={"head": 0}, device_id_type=MESH)
+
+    @pl.when(head == 0)
+    def _():
+        pl.semaphore_wait(greet_sem.at[1], 1)
 
     def summed(rows):
         while len(rows) > 1:
-            rows = [functools.reduce(lambda a, b: a + b, rows[i : i + 2]) for i in range(0, len(rows), 2)]
+            rows = [
+                functools.reduce(lambda a, b: a + b, rows[i : i + 2])
+                for i in range(0, len(rows), 2)
+            ]
         return rows[0]
 
-    @pl.when(head == 1)
-    def _():
-        pl.semaphore_wait(barrier, len(chips))
-        pl.semaphore_signal(greet_sem.at[1], inc=1, device_id={"head": 0}, device_id_type=MESH)
+    def first_copy(k, core):
+        tz, tx = targets_a[k]
+        return pltpu.make_async_remote_copy(
+            src_ref=send_a.at[pl.ds(2 * k, 2)],
+            dst_ref=recv_a.at[pl.ds(core * stretch + 2 * spot, 2)],
+            send_sem=ssem_a.at[k],
+            recv_sem=rsem_a.at[core * len(targets_a) + k],
+            device_id={"dp_1": tz, "dp_2": tx, "head": 1},
+            device_id_type=MESH,
+        )
+
+    stretch = 2 * plane + SLOTS + 1
+    for k in range(len(targets_a)):
+        send_a[2 * k] = rows_a[gives_a[k]]
+        send_a[2 * k + 1] = totals
+        first_copy(k, head).start()
+    rows_a[SLOTS] = totals
+    own_copy = pltpu.make_async_remote_copy(
+        src_ref=rows_a,
+        dst_ref=recv_a.at[pl.ds(2 * plane, SLOTS + 1)],
+        send_sem=own_sem.at[0],
+        recv_sem=own_sem.at[1],
+        device_id={"head": 1},
+        device_id_type=MESH,
+    )
 
     @pl.when(head == 0)
     def _():
-        pl.semaphore_wait(greet_sem.at[1], 1)
-
-    a_peers = [{"dp_1": tz, "dp_2": tx} for tz, tx in targets_a]
-    a_copies = exchange(a_peers, spot, plane, totals, rows_a, recv_a, send_a, ssem_a, rsem_a, gives_a)
+        own_copy.start()
+
     counted = len_v[...].astype(jnp.float32)
     tokens = jnp.sum(jnp.sum(counted, axis=0, keepdims=True), axis=1, keepdims=True)
     pairs = jnp.sum(jnp.sum(counted * counted, axis=0, keepdims=True), axis=1, keepdims=True)
-    for copy in a_copies:
-        copy.wait_recv()
-    for s in range(SLOTS):
-        rows_b[s] = recv_a[takes_a[s]]
-    totals = summed([recv_a[2 * i + 1] for i in range(plane)])
-
-    b_peers = [{"dp_0": (y + k) % ny} for k in range(1, ny)]
-    b_copies = exchange(b_peers, y, ny, totals, rows_b, recv_b, send_b, ssem_b, rsem_b, gives_b)
-    crosses = []
-    for k in range(ny):
-        copy = pltpu.make_async_remote_copy(
-            src_ref=send_b.at[pl.ds(1, 1)],
-            dst_ref=cross_b.at[pl.ds(y, 1)],
-            send_sem=ssem_c.at[k],
-            recv_sem=rsem_c.at[k],
-            device_id={"dp_0": (y + k) % ny, "head": away},
+
+    def second_copy(core, k):
+        return pltpu.make_async_remote_copy(
+            src_ref=send_b.at[pl.ds(2 * (core * (ny - 1) + k - 1), 2)],
+            dst_ref=recv_b.at[pl.ds(2 * y, 2)],
+            send_sem=ssem_b.at[core * (ny - 1) + k - 1],
+            recv_sem=rsem_b.at[k - 1],
+            device_id={"dp_0": (y + k) % ny, "head": core},
             device_id_type=MESH,
         )
-        copy.start()
-        crosses.append(copy)
-    for copy in map_copies + [hid_copy] + a_copies:
+
+    back_copy = pltpu.make_async_remote_copy(
+        src_ref=rows_b,
+        dst_ref=recv_b.at[pl.ds(2 * ny, SLOTS + 1)],
+        send_sem=own_sem.at[2],
+        recv_sem=own_sem.at[3],
+        device_id={"head": 0},
+        device_id_type=MESH,
+    )
+
+    @pl.when(head == 1)
+    def _():
+        for s in range(SLOTS + 1):
+            recv_a[stretch + 2 * plane + s] = rows_a[s]
+        own_copy.wait_recv()
+        for core in range(2):
+            recv_a[core * stretch + 2 * spot + 1] = recv_a[core * stretch + 2 * plane + SLOTS]
+        for core in range(2):
+            for k in range(len(targets_a)):
+                first_copy(k, core).wait_recv()
+        whole = summed(
+            [recv_a[core * stretch + 2 * i + 1] for core in range(2) for i in range(plane)]
+        )
+        for s in range(SLOTS):
+            rows_b[s] = recv_a[takes_a[s]]
+            rows_c[s] = recv_a[stretch + takes_a[s]]
+        for core in range(2):
+            rows = (rows_b, rows_c)[core]
+            for k in range(1, ny):
+                place = 2 * (core * (ny - 1) + k - 1)
+                send_b[place] = rows[gives_b[k - 1]]
+                send_b[place + 1] = whole
+                second_copy(core, k).start()
+        rows_b[SLOTS] = whole
+        back_copy.start()
+        for s in range(SLOTS):
+            recv_b[2 * ny + s] = rows_c[s]
+        recv_b[2 * ny + SLOTS] = whole
+
+    for copy in map_copies + [hid_copy]:
         copy.wait_send()
-    for copy in b_copies:
-        copy.wait_recv()
+    for k in range(len(targets_a)):
+        first_copy(k, head).wait_send()
+
+    @pl.when(head == 0)
+    def _():
+        own_copy.wait_send()
+        back_copy.wait_recv()
+
+    recv_b[2 * y + 1] = recv_b[2 * ny + SLOTS]
+    for k in range(1, ny):
+        second_copy(0, k).wait_recv()
     for s in range(SLOTS):
         row_out[s] = recv_b[takes_b[s]]
-    for copy in crosses:
-        copy.wait_recv()
-    same = summed([recv_b[2 * i + 1] for i in range(ny)])
-    cross = summed([cross_b[i] for i in range(ny)])
-    totals = same + cross
+    totals = summed([recv_b[2 * i + 1] for i in range(ny)])
     hidden_total = jnp.sum(totals[:, :128], axis=1, keepdims=True)
     attention_total = jnp.sum(totals[:, 128:], axis=1, keepdims=True)
     loss = hidden_total / tokens + attention_total / pairs
     loss_out[...] = jnp.broadcast_to(loss, loss_out.shape)
 
-    for copy in b_copies + crosses:
-        copy.wait_send()
+    @pl.when(head == 1)
+    def _():
+        for core in range(2):
+            for k in range(1, ny):
+                second_copy(core, k).wait_send()
+        back_copy.wait_send()
 
 
 def deliver(*refs):
@@ -431,11 +480,11 @@
         pltpu.VMEM((SLOTS, 1, HALF), f32),
         pltpu.VMEM((SLOTS, 1, HALF), f32),
         pltpu.VMEM((2 * (plane - 1), 1, HALF), f32),
-        pltpu.VMEM((2 * (ny - 1), 1, HALF), f32),
-        pltpu.VMEM((2 * plane + SLOTS, 1, HALF), f32),
-        pltpu.VMEM((2 * ny + SLOTS, 1, HALF), f32),
-        pltpu.VMEM((ny, 1, HALF), f32),
-        pltpu.VMEM((SLOTS, 1, HALF), f32),
+        pltpu.VMEM((4 * (ny - 1), 1, HALF), f32),
+        pltpu.VMEM((2 * (2 * plane + SLOTS + 1), 1, HALF), f32),
+        pltpu.VMEM((2 * ny + SLOTS + 1, 1, HALF), f32),
+        pltpu.VMEM((SLOTS + 1, 1, HALF), f32),
+        pltpu.VMEM((SLOTS + 1, 1, HALF), f32),
         pltpu.VMEM((SLOTS, 1, HALF), f32),
         dma((6 * SLOTS + 1 + 4 * SLOTS,)),
         dma((3,)),
@@ -443,11 +492,10 @@
         dma((SLOTS,)),
         dma((2,)),
         dma((plane - 1,)),
-        dma((plane - 1,)),
+        dma((2 * (plane - 1),)),
+        dma((2 * (ny - 1),)),
         dma((ny - 1,)),
-        dma((ny - 1,)),
-        dma((ny,)),
-        dma((ny,)),
+        dma((4,)),
         pltpu.SemaphoreType.REGULAR((2,)),
     ]
     shapes = ((2 * SLOTS, 128), (SLOTS, 1, HALF), (1, 128))

time: 27.4 us -> 27 us (0.985)
  Pallas kernels: 26.7 us -> 26.3 us
    pallas_call x1, Pallas kernels: 26.1 us -> 25.7 us  [body(): pl.pallas_call(functools.partial(kernel, sizes, bits), name='distill', ou...]
where the time goes in v4:
time: 27 us; the launch traced here: 26.9 us
  Pallas kernels  26.3 us (97%)
  between operations  0.64 us (2%)
    pallas_call x1, Pallas kernels, body(): pl.pallas_call(functools.partial(kernel, sizes, bits), name='distill', ou...  25.7 us
    pallas_call x1, Pallas kernels, body(): pl.pallas_call(deliver, name='deliver', out_shape=tuple((jax.ShapeDtypeSt...  0.63 us

profile of v4, /device:TPU:1, one launch (start us, length us, event | category | flops | bytes accessed | tf_op | source)
XLA Modules:
  0.0 26.9 jit_solution(4579801994833331884)
XLA Ops:
  0.6 25.7 %distill.1 = (f32[10,128]{1,0:T(8,128)S(1)}, f32[5,1,256]{2,1,0:T(1,128)S(1)}, f32[1,128]{1,0:T(1,128)S(1)}) custom-call(bf16[2560,512]{1,0:T(8,128)(2,1)} %th.1, bf16[312,2560]{1,0:T(8,128)(2,1)} %bitcast.10, bf16[312,512]{1,0:T(8,128)(2,1)} %pj.1, bf16[2560,512]{1,0:T(8,128)(2,1)} %tq.1, bf16[2560,512]{1,0:T(8,128)(2,1)} %tk.1, ...), custom_call_target="tpu_custom_call" | custom-call | flops 3500000000 | bytes 12000000 | tf_op jit(solution)/shard_map/distill/pallas_call | solution.py:502
  26.3 0.6 %deliver.1 = (f32[10,128]{1,0:T(8,128)}, f32[5,1,256]{2,1,0:T(1,128)}, f32[1,128]{1,0:T(1,128)}) custom-call(f32[10,128]{1,0:T(8,128)S(1)} %get-tuple-element.9.refs_0_, f32[5,1,256]{2,1,0:T(1,128)S(1)} %get-tuple-element.10.refs_1_, f32[1,128]{1,0:T(1,128)S(1)} %get-tuple-element.11.refs_2_), custom_call_target="tpu_custom_call" | custom-call | tf_op jit(solution)/shard_map/deliver/pallas_call | solution.py:516

commit v5 on v4

--- a/solution.py
+++ b/solution.py
@@ -197,12 +197,7 @@
 
     for copy in loads[1]:
         copy.start()
-    for copy in small:
-        copy.wait()
-    for copy in loads[2]:
-        copy.start()
-    gives_a, gives_b, takes_a, takes_b = routes()
-    for copy in loads[3]:
+    for copy in loads[2] + loads[3]:
         copy.start()
 
     ahead = {
@@ -242,6 +237,10 @@
             )
             copy.start()
             map_copies.append(copy)
+        if group == (0,):
+            for copy in small:
+                copy.wait()
+            gives_a, gives_b, takes_a, takes_b = routes()
 
     lane = lax.broadcasted_iota(jnp.int32, (1, HALF), 1)
     sublane = lax.broadcasted_iota(jnp.int32, (8, HALF), 0)

time: 27 us -> 26.8 us (level)
  no operation moved by 1% of the time
where the time goes in v5:
time: 26.8 us; the launch traced here: 26.7 us
  Pallas kernels  26.1 us (97%)
  between operations  0.64 us (2%)
    pallas_call x1, Pallas kernels, body(): pl.pallas_call(functools.partial(kernel, sizes, bits), name='distill', ou...  25.4 us
    pallas_call x1, Pallas kernels, body(): pl.pallas_call(deliver, name='deliver', out_shape=tuple((jax.ShapeDtypeSt...  0.63 us

profile of v5, /device:TPU:1, one launch (start us, length us, event | category | flops | bytes accessed | tf_op | source)
XLA Modules:
  0.0 26.7 jit_solution(18341550343435843882)
XLA Ops:
  0.6 25.4 %distill.1 = (f32[10,128]{1,0:T(8,128)S(1)}, f32[5,1,256]{2,1,0:T(1,128)S(1)}, f32[1,128]{1,0:T(1,128)S(1)}) custom-call(bf16[2560,512]{1,0:T(8,128)(2,1)} %th.1, bf16[312,2560]{1,0:T(8,128)(2,1)} %bitcast.10, bf16[312,512]{1,0:T(8,128)(2,1)} %pj.1, bf16[2560,512]{1,0:T(8,128)(2,1)} %tq.1, bf16[2560,512]{1,0:T(8,128)(2,1)} %tk.1, ...), custom_call_target="tpu_custom_call" | custom-call | flops 3500000000 | bytes 12000000 | tf_op jit(solution)/shard_map/distill/pallas_call | solution.py:501
  26.1 0.6 %deliver.1 = (f32[10,128]{1,0:T(8,128)}, f32[5,1,256]{2,1,0:T(1,128)}, f32[1,128]{1,0:T(1,128)}) custom-call(f32[10,128]{1,0:T(8,128)S(1)} %get-tuple-element.9.refs_0_, f32[5,1,256]{2,1,0:T(1,128)S(1)} %get-tuple-element.10.refs_1_, f32[1,128]{1,0:T(1,128)S(1)} %get-tuple-element.11.refs_2_), custom_call_target="tpu_custom_call" | custom-call | tf_op jit(solution)/shard_map/deliver/pallas_call | solution.py:515
